TPU v7x, 8 devices: a whole 2x2x1 slice. The times are simulated.
8 devices in a mesh: rep: 2 (over y, z), dp: 4 (over x, core).
Axes of the slice: x: 2, y: 2, z: 1, core: 2. Of those that a mesh axis runs over, the one named last changes fastest.
Arguments:
- x: bfloat16 [8, 2048, 1152], P(('rep', 'dp')), parts along dimension 0
- dy: bfloat16 [8, 2048, 1152], P(('rep', 'dp')), parts along dimension 0
- w_gate: bfloat16 [2, 1152, 4608], P(None, 'dp')
- w_up: bfloat16 [2, 1152, 4608], P(None, 'dp')
- w_down: bfloat16 [2, 4608, 1152], P(None, 'dp')
- m_w_gate: float32 [2, 1152, 4608], P(None, 'dp')
- m_w_up: float32 [2, 1152, 4608], P(None, 'dp')
- m_w_down: float32 [2, 4608, 1152], P(None, 'dp')
- v_w_gate: float32 [2, 1152, 4608], P(None, 'dp')
- v_w_up: float32 [2, 1152, 4608], P(None, 'dp')
- v_w_down: float32 [2, 4608, 1152], P(None, 'dp')
Outputs:
- output 1: bfloat16 [4, 1152, 4608], P('rep', 'dp'), parts along dimension 0
- output 2: bfloat16 [4, 1152, 4608], P('rep', 'dp'), parts along dimension 0
- output 3: bfloat16 [4, 4608, 1152], P('rep', 'dp'), parts along dimension 0
- output 4: float32 [4, 1152, 4608], P('rep', 'dp'), parts along dimension 0
- output 5: float32 [4, 1152, 4608], P('rep', 'dp'), parts along dimension 0
- output 6: float32 [4, 4608, 1152], P('rep', 'dp'), parts along dimension 0
- output 7: float32 [4, 1152, 4608], P('rep', 'dp'), parts along dimension 0
- output 8: float32 [4, 1152, 4608], P('rep', 'dp'), parts along dimension 0
- output 9: float32 [4, 4608, 1152], P('rep', 'dp'), parts along dimension 0
There are 2 independent parts. A program takes and returns all parts, laid end to end along the dimension named above; an argument that names none is the same for every part.
All inputs are finite; a program needn't handle non-finite values.
Results may differ from a plain program's by a relative error of at most 0.022.
Values are sent between devices in bfloat16 or wider.
A program may use at most 2 GiB of HBM per device.

v0:
```python
import jax
import jax.numpy as jnp
from jax import lax
from jax.sharding import PartitionSpec as P

NAMES = ("w_gate", "w_up", "w_down")


def matmul(a, w):
    return jnp.dot(a, w, preferred_element_type=jnp.float32).astype(jnp.bfloat16)


def normed(h):
    wide = h.astype(jnp.float32)
    scale = lax.rsqrt(jnp.mean(wide**2, -1, keepdims=True) + 1e-6)
    return (wide * scale).astype(jnp.bfloat16)


def layer(h, w):
    a = normed(h)
    gate = jnp.dot(a, w["w_gate"], preferred_element_type=jnp.float32)
    up = jnp.dot(a, w["w_up"], preferred_element_type=jnp.float32)
    return h + matmul((jax.nn.silu(gate) * up).astype(jnp.bfloat16), w["w_down"])


def adamw(w, m, v, g):
    m = 0.9 * m + 0.1 * g
    v = 0.95 * v + 0.05 * g * g
    step = m * lax.rsqrt(v + 1e-8) + 0.1 * w
    return (w - 0.02 * step).astype(jnp.bfloat16), m, v


def clipped(gradients, sum_of_squares, count):
    factor = jnp.minimum(1.0, 0.5 * lax.rsqrt(sum_of_squares / count + 1e-30))
    return [g * factor for g in gradients]


def solution(mesh):
    def fetched(weights, number):
        return {name: lax.all_gather(w[number], "dp", axis=0, tiled=True) for name, w in zip(NAMES, weights, strict=True)}

    def step(x, dy, *arrays):
        weights, m, v = (arrays[i : i + 3] for i in (0, 3, 6))
        layers = weights[0].shape[0]
        h, kept = x[0], []
        for number in range(layers):
            kept.append(h)
            h = layer(h, fetched(weights, number))
        by_h, mine = dy[0], [None] * layers
        for number in reversed(range(layers)):
            _, back = jax.vjp(lambda w, h: layer(h, w), fetched(weights, number), kept[number])
            by_w, by_h = back(by_h)
            mine[number] = [lax.psum_scatter(by_w[name], "dp", scatter_dimension=0, tiled=True) for name in NAMES]
        gradients = [jnp.stack([mine[number][i] for number in range(layers)]).astype(jnp.float32) for i in range(3)]
        squares = lax.psum(sum(jnp.sum(g * g) for g in gradients), "dp")
        gradients = clipped(gradients, squares, lax.psum(1, "dp") * sum(g.size for g in gradients))
        new = [adamw(w.astype(jnp.float32), m, v, g) for w, m, v, g in zip(weights, m, v, gradients, strict=True)]
        return tuple(one[which] for which in range(3) for one in new)

    states, cut = P(("rep", "dp"), None, None), P(None, "dp", None)
    return jax.shard_map(
        step,
        mesh=mesh,
        in_specs=(states, states) + (cut,) * 9,
        out_specs=(P("rep", "dp", None),) * 9,
        check_vma=False,
    )
```

profile of v0, /device:TPU:0, one launch (start us, length us, event | category | flops | bytes accessed | tf_op | source)
XLA Modules:
  0.0 1167.7 jit_solution(2686146430444993409)
XLA Ops:
  7.2 5.3 fusion.103
  12.5 0.0 all-gather.15.cloned.1.call-start
  12.6 5.3 fusion.102
  17.9 0.0 all-gather.17.cloned.1.call-start
  17.9 5.3 fusion.101
  23.3 0.5 all-gather.21.cloned.1.call-update
  23.9 0.5 all-gather.23.cloned.1.call-update
  24.5 0.5 all-gather.19.cloned.1.call-update
  25.1 6.6 copy.20
  31.7 3.3 fusion.55
  35.0 6.6 copy.21
  41.6 42.5 %all-gather.13.cloned.1.call-done = bf16[1,1152,4608]{2,1,0:T(8,128)(2,1)} async-done(((bf16[1,288,4608]{2,1,0:T(8,128)(2,1)}), bf16[1,1152,4608]{2,1,0:T(8,128)(2,1)}) %all-gather.13.cloned.1.call-update) | async-done | bytes 10616848 | tf_op jit(solution)/shard_map/all_gather | solution.py:40
  84.1 32.0 %fusion.53 = f32[2048,4608]{1,0:T(8,128)} fusion(bf16[1,1152,4608]{2,1,0:T(8,128)(2,1)} %all-gather.13.cloned.1.call-done, bf16[1,2048,1152]{1,2,0:T(8,128)(2,1)} %copy.20, f32[2048]{0:T(1024)S(1)} %add_rsqrt_fusion), kind=kOutput, calls=%fused_computation.87 | convolution fusion | flops 21750349824 | bytes 53092352 | tf_op jit(solution)/shard_map/dot_general | solution.py:21
  116.1 38.7 %all-gather.15.cloned.1.call-done = bf16[1,1152,4608]{2,1,0:T(8,128)(2,1)} async-done(((bf16[1,288,4608]{2,1,0:T(8,128)(2,1)}), bf16[1,1152,4608]{2,1,0:T(8,128)(2,1)}) %all-gather.15.cloned.1.call-update) | async-done | bytes 10616848 | tf_op jit(solution)/shard_map/all_gather | solution.py:40
  154.8 45.6 %multiply_convert_fusion.1 = (bf16[2048,4608]{1,0:T(8,128)(2,1)}, f32[2048,4608]{1,0:T(8,128)}) fusion(f32[2048,4608]{1,0:T(8,128)} %fusion.53, bf16[1,1152,4608]{2,1,0:T(8,128)(2,1)} %all-gather.15.cloned.1.call-done, bf16[1,2048,1152]{1,2,0:T(8,128)(2,1)} %copy.20, f32[2048]{0:T(1024)S(1)} %add_rsqrt_fusion), kind=kOutput, calls=%fused_computation.17 | convolution fusion | flops 21806972928 | bytes 109715456 | tf_op jit(solution)/shard_map/dot_general | solution.py:22
  200.4 25.1 %all-gather.17.cloned.1.call-done = bf16[1,4608,1152]{2,1,0:T(8,128)(2,1)} async-done(((bf16[1,1152,1152]{2,1,0:T(8,128)(2,1)}), bf16[1,4608,1152]{2,1,0:T(8,128)(2,1)}) %all-gather.17.cloned.1.call-update) | async-done | bytes 10616848 | tf_op jit(solution)/shard_map/all_gather | solution.py:40
  225.6 30.4 %fusion.59 = (f32[2048]{0:T(1024)S(1)}, bf16[2048,1152]{0,1:T(8,128)(2,1)}) fusion(bf16[2048,4608]{1,0:T(8,128)(2,1)} %get-tuple-element.24, bf16[1,4608,1152]{2,1,0:T(8,128)(2,1)} %all-gather.17.cloned.1.call-done, bf16[1,2048,1152]{1,2,0:T(8,128)(2,1)} %copy.20), kind=kOutput, calls=%fused_computation.93 | convolution fusion | flops 21755066368 | bytes 38936576 | tf_op jit(solution)/shard_map/dot_general | solution.py:10
  256.0 40.1 %all-gather.21.cloned.1.call-done = bf16[1,4608,1152]{2,1,0:T(8,128)(2,1)} async-done(((bf16[1,1152,1152]{2,1,0:T(8,128)(2,1)}), bf16[1,4608,1152]{2,1,0:T(8,128)(2,1)}) %all-gather.21.cloned.1.call-update) | async-done | bytes 10616848 | tf_op jit(solution)/shard_map/all_gather | solution.py:40
  296.1 31.5 %convolution_convert_fusion.1 = bf16[2048,4608]{1,0:T(8,128)(2,1)} fusion(bf16[1,4608,1152]{2,1,0:T(8,128)(2,1)} %all-gather.21.cloned.1.call-done, bf16[1,2048,1152]{2,1,0:T(8,128)(2,1)} %param.12), kind=kOutput, calls=%fused_computation.26 | convolution fusion | flops 21752709120 | bytes 34209792 | tf_op jit(solution)/shard_map/transpose(jvp())/dot_general | solution.py:10
  327.7 39.0 %all-gather.23.cloned.1.call-done = bf16[1,1152,4608]{2,1,0:T(8,128)(2,1)} async-done(((bf16[1,288,4608]{2,1,0:T(8,128)(2,1)}), bf16[1,1152,4608]{2,1,0:T(8,128)(2,1)}) %all-gather.23.cloned.1.call-update) | async-done | bytes 10616848 | tf_op jit(solution)/shard_map/all_gather | solution.py:40
  366.7 32.2 %fusion.40 = f32[2048,4608]{1,0:T(8,128)} fusion(bf16[1,1152,4608]{2,1,0:T(8,128)(2,1)} %all-gather.23.cloned.1.call-done, bf16[2048,1152]{0,1:T(8,128)(2,1)} %get-tuple-element.27, f32[2048]{0:T(1024)S(1)} %fusion.89), kind=kOutput, calls=%fused_computation.74 | convolution fusion | flops 21750349824 | bytes 53092352 | tf_op jit(solution)/shard_map/jvp()/dot_general | solution.py:22
  398.9 38.4 %all-gather.19.cloned.1.call-done = bf16[1,1152,4608]{2,1,0:T(8,128)(2,1)} async-done(((bf16[1,288,4608]{2,1,0:T(8,128)(2,1)}), bf16[1,1152,4608]{2,1,0:T(8,128)(2,1)}) %all-gather.19.cloned.1.call-update) | async-done | bytes 10616848 | tf_op jit(solution)/shard_map/all_gather | solution.py:40
  437.3 53.1 %fusion.2 = (bf16[2048,4608]{1,0:T(8,128)(2,1)}, f32[2048,4608]{1,0:T(8,128)}) fusion(f32[2048,4608]{1,0:T(8,128)} %fusion.40, bf16[2048,4608]{1,0:T(8,128)(2,1)} %convolution_convert_fusion.1, bf16[1,1152,4608]{2,1,0:T(8,128)(2,1)} %all-gather.19.cloned.1.call-done, bf16[2048,1152]{0,1:T(8,128)(2,1)} %get-tuple-element.27, f32[2048]{0:T(1024)S(1)} %fusion.89), kind=kOutput, calls=%fused_computation.8 | convolution fusion | flops 21863596032 | bytes 128589824 | tf_op jit(solution)/shard_map/jvp()/dot_general | solution.py:21
  490.4 29.3 %fusion.65 = bf16[2048,1152]{0,1:T(8,128)(2,1)} fusion(bf16[2048,4608]{1,0:T(8,128)(2,1)} %get-tuple-element.28, bf16[1,1152,4608]{2,1,0:T(8,128)(2,1)} %all-gather.19.cloned.1.call-done), kind=kOutput, calls=%fused_computation.97 | convolution fusion | flops 21743271936 | bytes 34209792 | tf_op jit(solution)/shard_map/transpose(jvp())/dot_general | solution.py:21
  519.7 38.2 %fusion.61 = (f32[2048]{0:T(1024)S(1)}, bf16[2048,1152]{0,1:T(8,128)(2,1)}) fusion(bf16[2048,1152]{0,1:T(8,128)(2,1)} %get-tuple-element.27, bf16[2048,1152]{0,1:T(8,128)(2,1)} %fusion.65, bf16[1,1152,4608]{2,1,0:T(8,128)(2,1)} %all-gather.23.cloned.1.call-done, bf16[2048,4608]{1,0:T(8,128)(2,1)} %convolution_convert_fusion.1, ...), kind=kOutput, calls=%fused_computation.95 | convolution fusion | flops 21814048768 | bytes 81403904 | tf_op jit(solution)/shard_map/transpose(jvp())/dot_general | solution.py:22
  558.0 8.6 fusion.78
  566.6 2.2 copy-done.1
  568.8 29.6 %convolution_convert_fusion.3 = bf16[4608,1152]{1,0:T(8,128)(2,1)} fusion(bf16[2048,4608]{1,0:T(8,128)(2,1)} %get-tuple-element.24, bf16[2048,1152]{0,1:T(8,128)(2,1)S(1)} %fusion.78), kind=kOutput, calls=%fused_computation.28 | convolution fusion | flops 21748580352 | bytes 34209792 | tf_op jit(solution)/shard_map/transpose(jvp())/dot_general | solution.py:10
  598.4 0.0 reduce-scatter.17.cloned.1.call-start
  598.5 37.6 %convolution_convert_fusion.2 = bf16[4608,1152]{1,0:T(8,128)(2,1)} fusion(f32[2048,4608]{1,0:T(8,128)} %fusion.40, bf16[1,2048,1152]{2,1,0:T(8,128)(2,1)} %param.12, f32[2048,4608]{1,0:T(8,128)} %get-tuple-element.29), kind=kOutput, calls=%fused_computation.27 | convolution fusion | flops 21805203456 | bytes 90832896 | tf_op jit(solution)/shard_map/transpose(jvp())/dot_general | solution.py:10
  636.1 0.0 reduce-scatter.11.cloned.1.call-start
  636.1 31.9 %convolution_convert_fusion = bf16[2048,4608]{1,0:T(8,128)(2,1)} fusion(bf16[2048,1152]{0,1:T(8,128)(2,1)} %copy-done.1, bf16[1,4608,1152]{2,1,0:T(8,128)(2,1)} %all-gather.17.cloned.1.call-done), kind=kOutput, calls=%fused_computation.25 | convolution fusion | flops 21752709120 | bytes 34209792 | tf_op jit(solution)/shard_map/transpose(jvp())/dot_general | solution.py:10
  668.1 34.5 %fusion.17 = bf16[1152,4608]{1,0:T(8,128)(2,1)} fusion(bf16[2048,4608]{1,0:T(8,128)(2,1)} %convolution_convert_fusion, f32[2048,4608]{1,0:T(8,128)} %fusion.53, bf16[1,2048,1152]{1,2,0:T(8,128)(2,1)} %copy.20, f32[2048]{0:T(1024)S(1)} %copy-done.7), kind=kOutput, calls=%fused_computation.24 | convolution fusion | flops 21812281344 | bytes 71966720 | tf_op jit(solution)/shard_map/transpose(jvp())/dot_general | solution.py:22
  702.6 0.0 reduce-scatter.13.cloned.1.call-start
  702.6 0.6 copy-done.3
  703.2 34.6 %fusion.13 = bf16[1152,4608]{1,0:T(8,128)(2,1)} fusion(bf16[2048,4608]{1,0:T(8,128)(2,1)} %convolution_convert_fusion.1, bf16[2048,1152]{0,1:T(8,128)(2,1)} %get-tuple-element.27, f32[2048]{0:T(1024)S(1)} %copy-done.3, f32[2048,4608]{1,0:T(8,128)} %get-tuple-element.29), kind=kOutput, calls=%fused_computation.22 | convolution fusion | flops 21812281344 | bytes 71966720 | tf_op jit(solution)/shard_map/transpose(jvp())/dot_general | solution.py:22
  737.9 41.8 %fusion.14 = bf16[1152,4608]{1,0:T(8,128)(2,1)} fusion(f32[2048,4608]{1,0:T(8,128)} %fusion.53, f32[2048,4608]{1,0:T(8,128)} %get-tuple-element.25, bf16[2048,4608]{1,0:T(8,128)(2,1)} %convolution_convert_fusion, bf16[1,2048,1152]{1,2,0:T(8,128)(2,1)} %copy.20, f32[2048]{0:T(1024)S(1)} %copy-done.7), kind=kOutput, calls=%fused_computation.23 | convolution fusion | flops 21859467264 | bytes 109715456 | tf_op jit(solution)/shard_map/transpose(jvp())/dot_general | solution.py:21
  779.8 28.8 %convolution_convert_fusion.4 = bf16[1152,4608]{1,0:T(8,128)(2,1)} fusion(bf16[2048,4608]{1,0:T(8,128)(2,1)} %get-tuple-element.28, bf16[2048,1152]{0,1:T(8,128)(2,1)} %get-tuple-element.27, f32[2048]{0:T(1024)S(1)} %copy-done.3), kind=kOutput, calls=%fused_computation.29 | convolution fusion | flops 21750349824 | bytes 34217984 | tf_op jit(solution)/shard_map/transpose(jvp())/dot_general | solution.py:21
  808.7 6.0 fusion.30
  814.7 26.5 %reduce-scatter.11.cloned.1.call-done = bf16[288,4608]{1,0:T(8,128)(2,1)} async-done(((bf16[1152,4608]{1,0:T(8,128)(2,1)}), bf16[288,4608]{1,0:T(8,128)(2,1)}) %reduce-scatter.11.cloned.1.call-update) | async-done | bytes 2654224 | tf_op jit(solution)/shard_map/reduce_scatter | solution.py:53
  841.2 81.7 %reduce-scatter.13.cloned.1.call-done = bf16[288,4608]{1,0:T(8,128)(2,1)} async-done(((bf16[1152,4608]{1,0:T(8,128)(2,1)}), bf16[288,4608]{1,0:T(8,128)(2,1)}) %reduce-scatter.13.cloned.1.call-update) | async-done | bytes 2654224 | tf_op jit(solution)/shard_map/reduce_scatter | solution.py:53
  922.9 5.9 fusion.29
  928.8 76.0 %reduce-scatter.7.cloned.1.call-done = bf16[288,4608]{1,0:T(8,128)(2,1)} async-done(((bf16[1152,4608]{1,0:T(8,128)(2,1)}), bf16[288,4608]{1,0:T(8,128)(2,1)}) %reduce-scatter.7.cloned.1.call-update) | async-done | bytes 2654224 | tf_op jit(solution)/shard_map/reduce_scatter | solution.py:53
  1004.8 81.7 %reduce-scatter.9.cloned.1.call-done = bf16[288,4608]{1,0:T(8,128)(2,1)} async-done(((bf16[1152,4608]{1,0:T(8,128)(2,1)}), bf16[288,4608]{1,0:T(8,128)(2,1)}) %reduce-scatter.9.cloned.1.call-update) | async-done | bytes 2654224 | tf_op jit(solution)/shard_map/reduce_scatter | solution.py:53
  1086.5 5.9 fusion.28
  1094.3 6.5 psum.7
  1101.6 21.6 %fusion.36 = (bf16[2,1152,1152]{2,1,0:T(8,128)(2,1)}, f32[2,1152,1152]{2,1,0:T(8,128)}, f32[2,1152,1152]{2,1,0:T(8,128)}) fusion(bf16[2,1152,1152]{2,1,0:T(8,128)(2,1)} %param.15, f32[]{:T(128)S(6)} %min_shard_map.3, bf16[1,1152,1152]{2,1,0:T(8,128)(2,1)} %bitcast.79, bf16[1,1152,1152]{2,1,0:T(8,128)(2,1)S(1)} %bitcast.77, f32[2,1152,1152]{2,1,0:T(8,128)} %param.21, ...), kind=kLoop, calls=%fused_computation.70 | loop fusion | flops 53084160 | bytes 58392580 | tf_op jit(solution)/shard_map/convert_element_type | solution.py:30
  1123.2 37.2 %fusion.27 = (bf16[2,288,4608]{2,1,0:T(8,128)(2,1)}, f32[2,288,4608]{2,1,0:T(8,128)}, f32[2,288,4608]{2,1,0:T(8,128)}, bf16[2,288,4608]{2,1,0:T(8,128)(2,1)}, f3...) fusion(bf16[2,288,4608]{2,1,0:T(8,128)(2,1)} %param.13, f32[]{:T(128)S(6)} %min_shard_map.3, ...), kind=kLoop, calls=%fused_computation.61 | loop fusion | flops 106168320 | bytes 116785152 | tf_op jit(solution)/shard_map/convert_element_type | solution.py:30
  (35 shorter events, 0.5 us)
Async XLA Ops:
  7.2 76.9 %all-gather.13.cloned.1.call-start = ((), (), s32[]{:S(2)}) async-start(), calls=%async_computation.12 | async-start | bytes 13271040 | tf_op jit(solution)/shard_map/all_gather | solution.py:40
  12.5 142.3 %all-gather.15.cloned.1.call-start = ((), (), s32[]{:S(2)}) async-start(), calls=%async_computation.13 | async-start | bytes 13271040 | tf_op jit(solution)/shard_map/all_gather | solution.py:40
  17.9 207.7 %all-gather.17.cloned.1.call-start = ((), (), s32[]{:S(2)}) async-start(), calls=%async_computation.14 | async-start | bytes 13271040 | tf_op jit(solution)/shard_map/all_gather | solution.py:40
  23.3 272.9 %all-gather.21.cloned.1.call-start = ((), (), s32[]{:S(2)}) async-start(), calls=%async_computation.16 | async-start | bytes 13271040 | tf_op jit(solution)/shard_map/all_gather | solution.py:40
  23.8 342.9 %all-gather.23.cloned.1.call-start = ((), (), s32[]{:S(2)}) async-start(), calls=%async_computation.17 | async-start | bytes 13271040 | tf_op jit(solution)/shard_map/all_gather | solution.py:40
  24.4 412.9 %all-gather.19.cloned.1.call-start = ((), (), s32[]{:S(2)}) async-start(), calls=%async_computation.15 | async-start | bytes 13271040 | tf_op jit(solution)/shard_map/all_gather | solution.py:40
  25.0 783.6 %reduce-scatter.15.cloned.1.call-start = ((), (), s32[]{:S(2)}) async-start(), calls=%async_computation.10 | async-start | bytes 13271040 | tf_op jit(solution)/shard_map/reduce_scatter | solution.py:53
  35.0 119.8 %copy-start.6 = (f32[2048]{0:T(1024)}, f32[2048]{0:T(1024)S(1)}, u32[]{:S(2)}) copy-start(f32[2048]{0:T(1024)S(1)} %add_rsqrt_fusion) | copy-start | bytes 24580
  256.0 71.7 %copy-start.4 = (f32[2048]{0:T(1024)}, f32[2048]{0:T(1024)S(1)}, u32[]{:S(2)}) copy-start(f32[2048]{0:T(1024)S(1)} %get-tuple-element.26) | copy-start | bytes 24580
  256.0 301.9 %copy-start.2 = (f32[2048]{0:T(1024)}, f32[2048]{0:T(1024)S(1)}, u32[]{:S(2)}) copy-start(f32[2048]{0:T(1024)S(1)} %fusion.89) | copy-start | bytes 24580
  519.7 38.3 %copy-start.5 = (f32[2048]{0:T(1024)S(1)}, f32[2048]{0:T(1024)}, u32[]{:S(2)}) copy-start(f32[2048]{0:T(1024)} %copy-done.4) | copy-start | bytes 24580
  566.6 2.2 copy-start.1
  598.4 210.2 %reduce-scatter.17.cloned.1.call-start = ((), (), s32[]{:S(2)}) async-start(), calls=%async_computation.11 | async-start | bytes 13271040 | tf_op jit(solution)/shard_map/reduce_scatter | solution.py:53
  636.1 32.0 %copy-start.7 = (f32[2048]{0:T(1024)S(1)}, f32[2048]{0:T(1024)}, u32[]{:S(2)}) copy-start(f32[2048]{0:T(1024)} %copy-done.6) | copy-start | bytes 24580
  636.1 205.1 %reduce-scatter.11.cloned.1.call-start = ((), (), s32[]{:S(2)}) async-start(), calls=%async_computation.8 | async-start | bytes 13271040 | tf_op jit(solution)/shard_map/reduce_scatter | solution.py:53
  702.5 0.7 copy-start.3
  702.6 220.4 %reduce-scatter.13.cloned.1.call-start = ((), (), s32[]{:S(2)}) async-start(), calls=%async_computation.9 | async-start | bytes 13271040 | tf_op jit(solution)/shard_map/reduce_scatter | solution.py:53
  737.9 266.9 %reduce-scatter.7.cloned.1.call-start = ((), (), s32[]{:S(2)}) async-start(), calls=%async_computation.6 | async-start | bytes 13271040 | tf_op jit(solution)/shard_map/reduce_scatter | solution.py:53
  779.7 306.7 %reduce-scatter.9.cloned.1.call-start = ((), (), s32[]{:S(2)}) async-start(), calls=%async_computation.7 | async-start | bytes 13271040 | tf_op jit(solution)/shard_map/reduce_scatter | solution.py:53
  808.6 292.9 %copy-start = (bf16[1152,1152]{1,0:T(8,128)(2,1)S(1)}, bf16[1152,1152]{1,0:T(8,128)(2,1)}, u32[]{:S(2)}) copy-start(bf16[1152,1152]{1,0:T(8,128)(2,1)} %reduce-scatter.15.cloned.1.call-done) | copy-start | bytes 7962628
Sparse Core Ops, SparseCore 0:
  12.6 71.4 all-gather.12
  86.2 68.5 all-gather.14
  156.9 68.5 all-gather.16
  227.5 68.5 all-gather.20
  298.1 68.5 all-gather.22
  368.7 68.5 all-gather.18
  598.5 78.9 reduce-scatter.14
  680.6 78.6 reduce-scatter.16
  762.5 78.6 reduce-scatter.10
  844.2 78.6 reduce-scatter.12
  926.1 78.6 reduce-scatter.6
  1007.8 78.6 reduce-scatter.8
where the time goes:
time: 1170 us
  matrix products  531 us (45%)
  waiting for transfers between devices  491 us (42%)
  other arithmetic  88.6 us (8%)
  local copies, waits for them, and re-layouts  31.9 us (3%)
  between operations  17.5 us (1%)
    reduce_scatter x6, waiting for transfers between devices, step(): lax.psum_scatter(by_w[name], 'dp', scatter_dimension=0, tiled=True)  266 us
    all_gather x6, waiting for transfers between devices, fetched(): lax.all_gather(w[number], 'dp', axis=0, tiled=True)  224 us
    dot_general x5, matrix products, layer(): up = jnp.dot(a, w['w_up'], preferred_element_type=jnp.float32)  185 us
    dot_general x5, matrix products, layer(): gate = jnp.dot(a, w['w_gate'], preferred_element_type=jnp.float32)  185 us
    dot_general x5, matrix products, matmul(): jnp.dot(a, w, preferred_element_type=jnp.float32).astype(jnp.bfloat16)  161 us
    convert_element_type x2, other arithmetic, adamw(): return ((w - 0.02 * step).astype(jnp.bfloat16), m, v)  58.8 us
  transfers between devices with their start and end apart: 12, of which 10 were waited for; matrix products, arithmetic and copies ran while one was open for 36% of the time, Pallas kernels for 0%

commit v1 on v0

v1 whole, which is shorter than its diff:
```python
import jax
import jax.numpy as jnp
from jax import lax
from jax.experimental import pallas as pl
from jax.experimental.pallas import tpu as pltpu
from jax.sharding import PartitionSpec as P

MESH = pl.DeviceIdType.MESH
T, D, FF, L = 2048, 1152, 4608, 2
BG, BD = D // 4, FF // 4
FQ = 1152
F32, BF16 = jnp.float32, jnp.bfloat16
ANY = pl.BlockSpec(memory_space=pl.ANY)


def nn(a, b):
    return lax.dot_general(a, b, (((1,), (0,)), ((), ())), preferred_element_type=F32)


def nt(a, b):
    return lax.dot_general(a, b, (((1,), (1,)), ((), ())), preferred_element_type=F32)


def tn(a, b):
    return lax.dot_general(a, b, (((0,), (0,)), ((), ())), preferred_element_type=F32)


def mega(x, dy, wg, wu, wd, *refs):
    (gg, gu, gd, sqg, sqd, GU, WD, A, AT, H1, HID, PRE, DG, DX, SC, RC, SX, RX, OWN, SCD, RCD, SXD, RXD, OWND, *sems) = refs
    ag_send, ag_recv, c_send, c_recv, x_send, x_recv, load_sem = sems
    r, d = lax.axis_index("rep"), lax.axis_index("dp")
    xx, cc = d // 2, d % 2
    dc, dx_, dxc = 2 * xx + 1 - cc, 2 * (1 - xx) + cc, 2 * (1 - xx) + 1 - cc
    to_c, to_x, to_y = (r, dc), (r, dx_), (1 - r, d)

    barrier = pltpu.get_barrier_semaphore()
    for to in (to_c, to_x, to_y):
        pl.semaphore_signal(barrier, inc=1, device_id=to, device_id_type=MESH)
    pl.semaphore_wait(barrier, 3)

    def remote(src, dst, s, q, to):
        return pltpu.make_async_remote_copy(src_ref=src, dst_ref=dst, send_sem=s, recv_sem=q, device_id=to, device_id_type=MESH)

    units = []
    for layer in range(L):
        for q in range(FF // FQ):
            cols = pl.ds(q * FQ, FQ)
            units.append([(wg, GU.at[layer, 0], layer, BG, 0, BG, cols), (wu, GU.at[layer, 1], layer, BG, 0, BG, cols)])
        for half in range(2):
            units.append([(wd, WD.at[layer], layer, BD, half * (BD // 2), BD // 2, pl.ds(0, D))])

    def flow(u, hop):
        out = []
        for i, (arg, full, layer, block, r0, rows, cols) in enumerate(units[u]):
            half = rows // 2
            mine = pl.ds(r0 + r * half, half)
            s, q = ag_send.at[u, i, hop], ag_recv.at[u, i, hop]
            if hop == 0:
                out.append(remote(arg.at[layer, mine, cols], full.at[pl.ds(d * block + r0 + r * half, half), cols], s, q, to_x))
            elif hop == 1:
                at = full.at[pl.ds(dx_ * block + r0 + r * half, half), cols]
                out.append(remote(at, at, s, q, to_y))
            elif hop == 2:
                out.append(remote(arg.at[layer, pl.ds(r0, rows), cols], full.at[pl.ds(d * block + r0, rows), cols], s, q, to_c))
            else:
                at = full.at[pl.ds(dx_ * block + r0, rows), cols]
                out.append(remote(at, at, s, q, to_c))
        return out

    def start(u, hop):
        for c in flow(u, hop):
            c.start()

    def arrive(u, hop):
        for c in flow(u, hop):
            c.wait_recv()

    n_units = len(units)
    for u in range(n_units):
        start(u, 0)
    for u in range(n_units):
        start(u, 2)

    def to_y_hop(u):
        if u < n_units:
            arrive(u, 0)
            start(u, 1)

    def to_c_hop(u):
        arrive(u, 1)
        start(u, 3)

    def whole(u):
        arrive(u, 2)
        arrive(u, 3)

    def load(dst, arg, full, layer, block, cols, base=0):
        out = [pltpu.make_async_copy(arg.at[layer, :, cols], dst.at[pl.ds(d * block, block), :], load_sem.at[base])]
        for i, b in enumerate((dc, dx_, dxc)):
            out.append(pltpu.make_async_copy(full.at[pl.ds(b * block, block), cols], dst.at[pl.ds(b * block, block), :], load_sem.at[base + 1 + i]))
        return out

    def run(copies):
        for c in copies:
            c.start()
        for c in copies:
            c.wait()

    def norm_of(h):
        wide = h.astype(F32)
        scale = lax.rsqrt(jnp.mean(wide * wide, -1, keepdims=True) + 1e-6)
        return wide * scale

    def norm_body(x_ref, a_ref, at_ref):
        a = norm_of(x_ref[...])
        a_ref[...] = a.astype(BF16)
        at_ref[...] = a.T.astype(BF16)

    def norm():
        b = 512
        pltpu.emit_pipeline(
            norm_body, grid=(T // b,), in_specs=[pl.BlockSpec((b, D), lambda i: (i, 0))],
            out_specs=[pl.BlockSpec((b, D), lambda i: (i, 0)), pl.BlockSpec((D, b), lambda i: (0, i))],
        )(x, A.at[0], AT.at[0])

    def gate_up(layer, q):
        def scoped(w):
            cols = pl.ds(q * FQ, FQ)
            run(load(w.at[0], wg, GU.at[layer, 0], layer, BG, cols) + load(w.at[1], wu, GU.at[layer, 1], layer, BG, cols, 4))

            def body(a_ref, gate_ref, up_ref, hid_ref):
                a = a_ref[...]
                gate, up = nn(a, w[0]), nn(a, w[1])
                gate_ref[...] = gate
                up_ref[...] = up
                hid_ref[...] = (gate * jax.nn.sigmoid(gate) * up).astype(BF16)

            b = 512
            out = pl.BlockSpec((b, FQ), lambda i: (i, q))
            pltpu.emit_pipeline(
                body, grid=(T // b,), in_specs=[pl.BlockSpec((b, D), lambda i: (i, 0))], out_specs=[out, out, out],
            )(A.at[layer], PRE.at[layer, 0], PRE.at[layer, 1], HID.at[layer])

        pl.run_scoped(scoped, pltpu.VMEM((2, D, FQ), BF16))

    def down():
        def scoped(w):
            run(load(w, wd, WD.at[0], 0, BD, pl.ds(0, D)))

            def body(x_ref, hid_ref, h_ref, a_ref, at_ref):
                h = x_ref[...] + nn(hid_ref[...], w[...]).astype(BF16)
                h_ref[...] = h
                a = norm_of(h)
                a_ref[...] = a.astype(BF16)
                at_ref[...] = a.T.astype(BF16)

            b = 256
            row = pl.BlockSpec((b, D), lambda i: (i, 0))
            pltpu.emit_pipeline(
                body, grid=(T // b,), in_specs=[row, pl.BlockSpec((b, FF), lambda i: (i, 0))],
                out_specs=[row, row, pl.BlockSpec((D, b), lambda i: (0, i))],
            )(x, HID.at[0], H1, A.at[1], AT.at[1])

        pl.run_scoped(scoped, pltpu.VMEM((FF, D), BF16))

    def by_hidden(layer):
        by = dy if layer else DX

        def scoped(w):
            run(load(w, wd, WD.at[layer], layer, BD, pl.ds(0, D)))

            def body(by_ref, gate_ref, up_ref, bg_ref, bu_ref):
                j = pl.program_id(1)
                rows = pl.ds(pl.multiple_of(j * FQ, FQ), FQ)
                by_hid = nt(by_ref[...], w[rows, :]).astype(BF16).astype(F32)
                gate, up = gate_ref[...], up_ref[...]
                s = jax.nn.sigmoid(gate)
                silu = gate * s
                bu_ref[...] = (by_hid * silu).astype(BF16)
                bg_ref[...] = (by_hid * up * (s + silu * (1 - s))).astype(BF16)

            b = 512
            tile = pl.BlockSpec((b, FQ), lambda i, j: (i, j))
            pltpu.emit_pipeline(
                body, grid=(T // b, FF // FQ), in_specs=[pl.BlockSpec((b, D), lambda i, j: (i, 0)), tile, tile],
                out_specs=[tile, tile],
            )(by, PRE.at[layer, 0], PRE.at[layer, 1], DG.at[layer, 0], DG.at[layer, 1])

        pl.run_scoped(scoped, pltpu.VMEM((FF, D), BF16))

    def by_input():
        def scoped(wg_, wu_):
            every = pl.ds(0, FF)
            run(load(wg_, wg, GU.at[1, 0], 1, BG, every) + load(wu_, wu, GU.at[1, 1], 1, BG, every, 4))

            def body(bg_ref, bu_ref, h_ref, dy_ref, out_ref):
                by_a = nt(bg_ref[...], wg_[...]).astype(BF16).astype(F32) + nt(bu_ref[...], wu_[...]).astype(BF16).astype(F32)
                by_a = by_a.astype(BF16).astype(F32)
                wide = h_ref[...].astype(F32)
                scale = lax.rsqrt(jnp.mean(wide * wide, -1, keepdims=True) + 1e-6)
                along = jnp.mean(by_a * wide, -1, keepdims=True)
                by_h = by_a * scale - wide * (scale * scale * scale * along)
                out_ref[...] = dy_ref[...] + by_h.astype(BF16)

            b = 256
            row, wide_row = pl.BlockSpec((b, D), lambda i: (i, 0)), pl.BlockSpec((b, FF), lambda i: (i, 0))
            pltpu.emit_pipeline(
                body, grid=(T // b,), in_specs=[wide_row, wide_row, row, row], out_specs=[row],
            )(DG.at[1, 0], DG.at[1, 1], H1, dy, DX)

        pl.run_scoped(scoped, pltpu.VMEM((D, FF), BF16), pltpu.VMEM((D, FF), BF16))

    def send_c(i):
        s, q = (SC, RC) if i < 4 else (SCD, RCD)
        k = i if i < 4 else i - 4
        return remote(s.at[k], q.at[k], c_send.at[i], c_recv.at[i], to_c)

    def send_x(i):
        s, q = (SX, RX) if i < 4 else (SXD, RXD)
        k = i if i < 4 else i - 4
        return remote(s.at[k], q.at[k], x_send.at[i], x_recv.at[i], to_x)

    def grad_gu(layer, m, first):
        i = 2 * layer + m

        def scoped(lhs):
            one, two = (dxc, dc) if first else (dx_, d)
            run([
                pltpu.make_async_copy(AT.at[layer, pl.ds(one * BG, BG), :], lhs.at[pl.ds(0, BG), :], load_sem.at[0]),
                pltpu.make_async_copy(AT.at[layer, pl.ds(two * BG, BG), :], lhs.at[pl.ds(BG, BG), :], load_sem.at[1]),
            ])
            b = 512
            by = pl.BlockSpec((T, b), lambda j: (0, j))
            both = pl.BlockSpec((2, BG, b), lambda j: (0, 0, j))
            single = pl.BlockSpec((BG, b), lambda j: (0, j))
            if first:
                def body(by_ref, out_ref):
                    g = nn(lhs[...], by_ref[...]).astype(BF16)
                    out_ref[0] = g[:BG]
                    out_ref[1] = g[BG:]

                pltpu.emit_pipeline(body, grid=(FF // b,), in_specs=[by], out_specs=[both])(DG.at[layer, m], SC.at[i])
            else:
                def body(by_ref, came_ref, x_ref, own_ref):
                    g = nn(lhs[...], by_ref[...]).astype(BF16).astype(F32)
                    x_ref[...] = (g[:BG] + came_ref[0].astype(F32)).astype(BF16)
                    own_ref[...] = g[BG:] + came_ref[1].astype(F32)

                pltpu.emit_pipeline(body, grid=(FF // b,), in_specs=[by, both], out_specs=[single, single])(
                    DG.at[layer, m], RC.at[i], SX.at[i], OWN.at[i])

        pl.run_scoped(scoped, pltpu.VMEM((2 * BG, T), BF16))

    def grad_d(layer, first):
        by = dy if layer else DX
        core = 1 - cc if first else cc

        def scoped(rhs):
            run([pltpu.make_async_copy(by, rhs, load_sem.at[0])])
            b = 384
            n = BD // b

            def hid_at(k, j):
                block = 2 * ((1 - xx) * (1 - k) + xx * k) + core
                return 0, block * n + j

            hid = pl.BlockSpec((T, b), hid_at)
            out = pl.BlockSpec((1, b, D), lambda k, j: (k, j, 0))
            if first:
                def body(hid_ref, out_ref):
                    out_ref[0] = tn(hid_ref[...], rhs[...]).astype(BF16)

                pltpu.emit_pipeline(body, grid=(2, n), in_specs=[hid], out_specs=[out])(HID.at[layer], SCD.at[layer])
            else:
                def one(k, outs):
                    def body(hid_ref, came_ref, out_ref):
                        g = tn(hid_ref[...], rhs[...]).astype(BF16).astype(F32) + came_ref[...].astype(F32)
                        out_ref[...] = g.astype(out_ref.dtype)

                    row = pl.BlockSpec((b, D), lambda j: (j, 0))
                    pltpu.emit_pipeline(
                        body, grid=(n,), in_specs=[pl.BlockSpec((T, b), lambda j: hid_at(k, j)), row], out_specs=[row],
                    )(HID.at[layer], RCD.at[layer, k], outs)

                one(0, SXD.at[layer])
                send_x(4 + layer).start()
                one(1, OWND.at[layer])

        pl.run_scoped(scoped, pltpu.VMEM((T, D), BF16))

    def finish(i, total, first):
        send_x(i).wait_recv()
        own, came, out = (OWN.at[i], RX.at[i], (gg, gu)[i % 2].at[i // 2]) if i < 4 else (OWND.at[i - 4], RXD.at[i - 4], gd.at[i - 4])
        rows, cols = (BG, FF) if i < 4 else (BD, D)
        b = 96 if i < 4 else 384
        if first:
            total[...] = jnp.zeros_like(total)

        def body(own_ref, came_ref, out_ref):
            g = (own_ref[...] + came_ref[...].astype(F32)).astype(BF16)
            out_ref[...] = g
            g = g.astype(F32)
            total[...] += jnp.sum((g * g).reshape(b // 8, 8, cols), axis=0)

        row = pl.BlockSpec((b, cols), lambda j: (j, 0))
        pltpu.emit_pipeline(body, grid=(rows // b,), in_specs=[row, row], out_specs=[row])(own, came, out)

    norm()
    to_y_hop(0)
    to_y_hop(1)
    step = 0

    def usable(u):
        to_c_hop(u)
        to_y_hop(u + 2)
        whole(u)

    for q in range(4):
        usable(q)
        gate_up(0, q)
    usable(4)
    usable(5)
    down()
    for q in range(4):
        usable(6 + q)
        gate_up(1, q)
    grad_d(1, True)
    send_c(5).start()
    usable(10)
    usable(11)
    send_c(5).wait_recv()
    grad_d(1, False)
    by_hidden(1)
    grad_gu(1, 0, True)
    send_c(2).start()
    grad_gu(1, 1, True)
    send_c(3).start()
    send_c(2).wait_recv()
    grad_gu(1, 0, False)
    send_x(2).start()
    send_c(3).wait_recv()
    grad_gu(1, 1, False)
    send_x(3).start()
    by_input()
    grad_d(0, True)
    send_c(4).start()
    by_hidden(0)
    send_c(4).wait_recv()
    grad_d(0, False)
    grad_gu(0, 0, True)
    send_c(0).start()
    grad_gu(0, 1, True)
    send_c(1).start()
    send_c(0).wait_recv()
    grad_gu(0, 0, False)
    send_x(0).start()
    send_c(1).wait_recv()
    grad_gu(0, 1, False)
    send_x(1).start()
    for n, i in enumerate((5, 4)):
        finish(i, sqd, n == 0)
    for n, i in enumerate((2, 3, 0, 1)):
        finish(i, sqg, n == 0)
    for u in range(n_units):
        for hop in range(4):
            for c in flow(u, hop):
                c.wait_send()
    for i in range(6):
        send_c(i).wait_send()
        send_x(i).wait_send()


def fused(x, dy, wg, wu, wd):
    def hbm(shape, dtype):
        return jax.ShapeDtypeStruct(shape, dtype)

    outs = [
        hbm((L, BG, FF), BF16), hbm((L, BG, FF), BF16), hbm((L, BD, D), BF16), hbm((8, FF), F32), hbm((8, D), F32),
        hbm((L, 2, D, FF), BF16), hbm((L, FF, D), BF16), hbm((L, T, D), BF16), hbm((L, D, T), BF16), hbm((T, D), BF16), hbm((L, T, FF), BF16),
        hbm((L, 2, T, FF), F32), hbm((L, 2, T, FF), BF16), hbm((T, D), BF16),
        hbm((4, 2, BG, FF), BF16), hbm((4, 2, BG, FF), BF16), hbm((4, BG, FF), BF16), hbm((4, BG, FF), BF16), hbm((4, BG, FF), F32),
        hbm((2, 2, BD, D), BF16), hbm((2, 2, BD, D), BF16), hbm((2, BD, D), BF16), hbm((2, BD, D), BF16), hbm((2, BD, D), F32),
    ]
    specs = [ANY] * len(outs)
    specs[3] = specs[4] = pl.BlockSpec(memory_space=pltpu.VMEM)
    dma = pltpu.SemaphoreType.DMA
    return pl.pallas_call(
        mega,
        out_shape=outs,
        in_specs=[ANY] * 5,
        out_specs=specs,
        scratch_shapes=[dma((12, 2, 4)), dma((12, 2, 4)), dma((6,)), dma((6,)), dma((6,)), dma((6,)), dma((8,))],
        compiler_params=pltpu.CompilerParams(collective_id=0, has_side_effects=True, vmem_limit_bytes=60 * 2**20),
        name="step",
    )(x, dy, wg, wu, wd)[:5]


def adamw(w, m, v, g):
    m = 0.9 * m + 0.1 * g
    v = 0.95 * v + 0.05 * g * g
    step = m * lax.rsqrt(v + 1e-8) + 0.1 * w
    return (w - 0.02 * step).astype(BF16), m, v


def solution(mesh):
    def step(x, dy, *arrays):
        weights, m, v = (arrays[i : i + 3] for i in (0, 3, 6))
        *gradients, sqg, sqd = fused(x[0], dy[0], *weights)
        squares = lax.psum(jnp.sum(sqg) + jnp.sum(sqd), "dp")
        count = lax.psum(1, "dp") * sum(g.size for g in gradients)
        factor = jnp.minimum(1.0, 0.5 * lax.rsqrt(squares / count + 1e-30))
        new = [adamw(w.astype(F32), m, v, g.astype(F32) * factor) for w, m, v, g in zip(weights, m, v, gradients, strict=True)]
        return tuple(one[which] for which in range(3) for one in new)

    states, cut = P(("rep", "dp"), None, None), P(None, "dp", None)
    return jax.shard_map(
        step,
        mesh=mesh,
        in_specs=(states, states) + (cut,) * 9,
        out_specs=(P("rep", "dp", None),) * 9,
        check_vma=False,
    )
```

time: 1170 us -> 881 us (0.75)
  Pallas kernels: 0 us -> 796 us
  matrix products: 531 us -> 0 us
  waiting for transfers between devices: 491 us -> 0 us
  local copies, waits for them, and re-layouts: 31.9 us -> 0 us
  other arithmetic: 88.6 us -> 64.7 us
  between operations: 17.5 us -> 3.1 us
    pallas_call x0 -> x1, Pallas kernels: none -> 796 us  [fused(): pl.pallas_call(mega, out_shape=outs, in_specs=[ANY] * 5, out_specs=specs,...]
    dot_general x15 -> x0, matrix products: 531 us -> none  [the longest x5 185 us: layer(): up = jnp.dot(a, w['w_up'], preferred_element_type=jnp.float32)]
    reduce_scatter x6 -> x0, waiting for transfers between devices: 266 us -> none  [step(): lax.psum_scatter(by_w[name], 'dp', scatter_dimension=0, tiled=True)]
    all_gather x6 -> x0, waiting for transfers between devices: 224 us -> none  [fetched(): lax.all_gather(w[number], 'dp', axis=0, tiled=True)]
    reduce_sum x4 -> x2, other arithmetic: 21.1 us -> 2.93 us  [step(): squares = lax.psum(jnp.sum(sqg) + jnp.sum(sqd), 'dp')]
    unnamed x18 -> x0, local copies, waits for them, and re-layouts: 16.1 us -> none
    slice x3 -> x0, local copies, waits for them, and re-layouts: 15.9 us -> none  [fetched(): w[number]]
  transfers between devices with their start and end apart: 12 -> 0, of which waited for: 10 -> 0; matrix products, arithmetic and copies ran while one was open for 36% -> 0% of each run, Pallas kernels for 0% -> 0%
where the time goes in v1:
time: 881 us; the launch traced here: 871 us
  Pallas kernels  796 us (90%)
  other arithmetic  64.7 us (7%)
    pallas_call x1, Pallas kernels, fused(): pl.pallas_call(mega, out_shape=outs, in_specs=[ANY] * 5, out_specs=specs,...  796 us
    convert_element_type x2, other arithmetic, adamw(): return ((w - 0.02 * step).astype(BF16), m, v)  61.8 us

profile of v1, /device:TPU:0, one launch (start us, length us, event | category | flops | bytes accessed | tf_op | source)
XLA Modules:
  0.0 870.9 jit_solution(15950750419820772567)
XLA Ops:
  0.6 795.5 %step.1 = (bf16[2,288,4608]{2,1,0:T(8,128)(2,1)}, bf16[2,288,4608]{2,1,0:T(8,128)(2,1)}, bf16[2,1152,1152]{2,1,0:T(8,128)(2,1)}, f32[8,4608]{1,0:T(8,128)}, f32[...) custom-call(bf16[2048,1152]{1,0:T(8,128)(2,1)} %bitcast.2, ...), custom_call_target="tpu_custom_call" | custom-call | tf_op jit(solution)/shard_map/step/pallas_call | solution.py:387
  796.2 1.4 reduce_sum.19
  797.6 1.6 reduce_sum.18
  800.4 7.6 psum.7
  808.7 22.1 %fusion.8 = (bf16[2,1152,1152]{2,1,0:T(8,128)(2,1)}, f32[2,1152,1152]{2,1,0:T(8,128)}, f32[2,1152,1152]{2,1,0:T(8,128)}) fusion(bf16[2,1152,1152]{2,1,0:T(8,128)(2,1)} %wd.1, f32[]{:T(128)S(6)} %min_shard_map.3, bf16[2,1152,1152]{2,1,0:T(8,128)(2,1)} %get-tuple-element.18, f32[2,1152,1152]{2,1,0:T(8,128)} %param.21, f32[2,1152,1152]{2,1,0:T(8,128)} %param.18), kind=kLoop, calls=%fused_computation.17 | loop fusion | flops 45121536 | bytes 58392580 | tf_op jit(solution)/shard_map/convert_element_type | solution.py:402
  830.8 39.6 %fusion.2 = (bf16[2,288,4608]{2,1,0:T(8,128)(2,1)}, f32[2,288,4608]{2,1,0:T(8,128)}, f32[2,288,4608]{2,1,0:T(8,128)}, bf16[2,288,4608]{2,1,0:T(8,128)(2,1)}, f32...) fusion(bf16[2,288,4608]{2,1,0:T(8,128)(2,1)} %wg.1, f32[]{:T(128)S(6)} %min_shard_map.3, ...), kind=kLoop, calls=%fused_computation.11 | loop fusion | flops 90243072 | bytes 116785152 | tf_op jit(solution)/shard_map/convert_element_type | solution.py:402

commit v2 on v0

v2 whole, which is shorter than its diff:
```python
import jax
import jax.numpy as jnp
from jax import lax
from jax.experimental import pallas as pl
from jax.experimental.pallas import tpu as pltpu
from jax.sharding import PartitionSpec as P

MESH = pl.DeviceIdType.MESH
T, D, FF, L = 2048, 1152, 4608, 2
BG, BD = D // 4, FF // 4
FU = 768
NU = FF // FU
F32, BF16 = jnp.float32, jnp.bfloat16
ANY = pl.BlockSpec(memory_space=pl.ANY)


def nn(a, b):
    return lax.dot_general(a, b, (((1,), (0,)), ((), ())), preferred_element_type=F32)


def nt(a, b):
    return lax.dot_general(a, b, (((1,), (1,)), ((), ())), preferred_element_type=F32)


def tn(a, b):
    return lax.dot_general(a, b, (((0,), (0,)), ((), ())), preferred_element_type=F32)


def mega(x, dy, wg, wu, wd, *refs):
    (gg, gu, gd, sq, GU, WD, AT, H1, HID, PRE, DH, DG, SC, RC, SX, RX, OWN, SCD, RCD, SXD, RXD, OWND) = refs[:22]
    (wgu, wdv, a_all, by_all, tot_g, tot_d, sq_all) = refs[22:29]
    (gs, gr, ds_, dr, c_send, c_recv, x_send, x_recv, sq_send, sq_recv, load_sem, wd_sem, by_sem) = refs[29:]
    r, d = lax.axis_index("rep"), lax.axis_index("dp")
    xx, cc = d // 2, d % 2
    dc, dx_, dxc = 2 * xx + 1 - cc, 2 * (1 - xx) + cc, 2 * (1 - xx) + 1 - cc
    to_c, to_x, to_xc, to_y = (r, dc), (r, dx_), (r, dxc), (1 - r, d)

    barrier = pltpu.get_barrier_semaphore()
    for to in (to_c, to_x, to_xc, to_y):
        pl.semaphore_signal(barrier, inc=1, device_id=to, device_id_type=MESH)
    pl.semaphore_wait(barrier, 4)

    def remote(src, dst, s, q, to):
        return pltpu.make_async_remote_copy(src_ref=src, dst_ref=dst, send_sem=s, recv_sem=q, device_id=to, device_id_type=MESH)

    def piece(arg, full, layer, block, r0, rows, cols, s, q, hop):
        half = rows // 2
        if hop == 0:
            mine = r0 + r * half
            return remote(arg.at[layer, pl.ds(mine, half), cols], full.at[pl.ds(d * block + mine, half), cols], s, q, to_x)
        if hop == 1:
            at = full.at[pl.ds(dx_ * block + r0 + r * half, half), cols]
            return remote(at, at, s, q, to_y)
        if hop == 2:
            return remote(arg.at[layer, pl.ds(r0, rows), cols], full.at[pl.ds(d * block + r0, rows), cols], s, q, to_c)
        at = full.at[pl.ds(dx_ * block + r0, rows), cols]
        return remote(at, at, s, q, to_c)

    def columns(u):
        return pl.ds(u * FU if isinstance(u, int) else pl.multiple_of(u * FU, FU), FU)

    class Gate:
        def __init__(self, layer, u):
            self.layer, self.u = layer, u

        def copies(self, hop):
            layer, u = self.layer, self.u
            return [piece(arg, GU.at[layer, m], layer, BG, 0, BG, columns(u), gs.at[layer, u, m, hop], gr.at[layer, u, m, hop], hop)
                    for m, arg in enumerate((wg, wu))]

    class Down:
        def __init__(self, layer, u):
            self.layer, self.u = layer, u

        def copies(self, hop):
            layer, u = self.layer, self.u
            return [piece(wd, WD.at[layer], layer, BD, u * (BD // 2), BD // 2, pl.ds(0, D), ds_.at[layer, u, hop], dr.at[layer, u, hop], hop)]

    def start(unit, hop):
        for c in unit.copies(hop):
            c.start()

    def arrive(unit, hop):
        for c in unit.copies(hop):
            c.wait_recv()

    def on_y(unit):
        arrive(unit, 0)
        start(unit, 1)

    def on_c(unit):
        arrive(unit, 1)
        start(unit, 3)

    def whole(unit):
        arrive(unit, 2)
        arrive(unit, 3)

    every = [Gate(0, u) for u in range(NU)] + [Down(0, 0), Down(0, 1), Down(1, 0), Down(1, 1)] + [Gate(1, u) for u in range(NU)]
    for unit in every:
        start(unit, 0)
    for unit in every:
        start(unit, 2)
    pltpu.make_async_copy(dy, by_all, by_sem).start()

    def gate_loads(layer, u):
        out = []
        for m, arg in enumerate((wg, wu)):
            for i, b in enumerate((d, dc, dx_, dxc)):
                rows = pl.ds(b * BG, BG)
                src = GU.at[layer, m, rows, columns(u)] if i else arg.at[layer, :, columns(u)]
                out.append(pltpu.make_async_copy(src, wgu.at[m, rows, columns(u)], load_sem.at[m, i]))
        return out

    def down_loads(layer):
        out = []
        for i, b in enumerate((d, dc, dx_, dxc)):
            rows = pl.ds(b * BD, BD)
            out.append(pltpu.make_async_copy(WD.at[layer, rows, :] if i else wd.at[layer], wdv.at[rows, :], wd_sem.at[b]))
        return out

    def begin(copies):
        for c in copies:
            c.start()

    def end(copies):
        for c in copies:
            c.wait()

    def down_here(layer, b):
        rows = pl.ds(b * BD, BD)
        pltpu.make_async_copy(WD.at[layer, rows, :], wdv.at[rows, :], wd_sem.at[b]).wait()

    def norm_of(h):
        wide = h.astype(F32)
        scale = lax.rsqrt(jnp.mean(wide * wide, -1, keepdims=True) + 1e-6)
        return wide * scale

    def rows_of(i, b):
        return pl.ds(pl.multiple_of(i * b, b), b)

    def at_steps(step, hooks):
        for when, what in hooks.items():

            @pl.when(step == when)
            def _(what=what):
                what()

    def norm():
        b = 512

        def body(x_ref, at_ref):
            a = norm_of(x_ref[...])
            a_all[rows_of(pl.program_id(0), b), :] = a.astype(BF16)
            at_ref[...] = a.T.astype(BF16)

        pltpu.emit_pipeline(
            body, grid=(T // b,), in_specs=[pl.BlockSpec((b, D), lambda i: (i, 0))], out_specs=[pl.BlockSpec((D, b), lambda i: (0, i))],
        )(x, AT.at[0])

    def gate_up(layer):
        b = 1024

        def body(*tiles):
            u, t = pl.program_id(0), pl.program_id(1)

            @pl.when(t == 0)
            def _():
                if layer == 0:
                    whole(Gate(layer, u))
                    begin(gate_loads(layer, u))
                end(gate_loads(layer, u))

            @pl.when(t == 1)
            def _():
                if layer == 0:
                    pl.when(u + 2 < NU)(lambda: on_y(Gate(0, u + 2)))
                    pl.when(u + 2 == NU)(lambda: on_y(Down(0, 0)))
                    pl.when(u + 1 < NU)(lambda: on_c(Gate(0, u + 1)))
                else:
                    at_steps(u, {0: lambda: (on_y(Gate(1, 5)), on_c(Gate(1, 3))), 1: lambda: on_c(Gate(1, 4)), 2: lambda: on_c(Gate(1, 5))})

                    @pl.when(u + 1 < NU)
                    def _():
                        whole(Gate(layer, u + 1))
                        begin(gate_loads(layer, u + 1))

            a = a_all[rows_of(t, b), :]
            gate, up = nn(a, wgu[0, :, columns(u)]), nn(a, wgu[1, :, columns(u)])
            s = jax.nn.sigmoid(gate)
            silu = gate * s
            if layer == 0:
                gate_ref, up_ref, hid_ref = tiles
                gate_ref[...] = gate
                up_ref[...] = up
            else:
                by_ref, hid_ref, bg_ref, bu_ref = tiles
                by_hid = by_ref[...].astype(F32)
                bu_ref[...] = (by_hid * silu).astype(BF16)
                bg_ref[...] = (by_hid * up * (s + silu * (1 - s))).astype(BF16)
            hid_ref[...] = (silu * up).astype(BF16)

        tile = pl.BlockSpec((b, FU), lambda u, t: (t, u))
        if layer == 0:
            pltpu.emit_pipeline(body, grid=(NU, T // b), in_specs=[], out_specs=[tile] * 3)(PRE.at[0], PRE.at[1], HID.at[0])
        else:
            pltpu.emit_pipeline(body, grid=(NU, T // b), in_specs=[tile], out_specs=[tile] * 3)(DH, HID.at[1], DG.at[1, 0], DG.at[1, 1])

    def down():
        b = 256

        def body(x_ref, hid_ref, h_ref, at_ref):
            i = pl.program_id(0)
            at_steps(i, {
                3: lambda: (on_y(Down(1, 1)), on_c(Down(1, 0))),
                6: lambda: on_y(Gate(1, 0)),
                7: lambda: on_c(Down(1, 1)),
            })
            h = x_ref[...] + nn(hid_ref[...], wdv[...]).astype(BF16)
            h_ref[...] = h
            a = norm_of(h)
            a_all[rows_of(i, b), :] = a.astype(BF16)
            at_ref[...] = a.T.astype(BF16)

        row = pl.BlockSpec((b, D), lambda i: (i, 0))
        pltpu.emit_pipeline(
            body, grid=(T // b,), in_specs=[row, pl.BlockSpec((b, FF), lambda i: (i, 0))],
            out_specs=[row, pl.BlockSpec((D, b), lambda i: (0, i))],
        )(x, HID.at[0], H1, AT.at[1])

    def by_hidden_1():
        b = 1024

        def body(out_ref):
            j, t = pl.program_id(0), pl.program_id(1)
            step = 2 * j + t
            at_steps(step, {
                0: lambda: down_here(1, 0),
                1: lambda: on_y(Gate(1, 1)),
                2: lambda: (down_here(1, 1), on_c(Gate(1, 0))),
                4: lambda: on_y(Gate(1, 2)),
                6: lambda: (down_here(1, 2), on_c(Gate(1, 1))),
                7: lambda: on_y(Gate(1, 3)),
                8: lambda: down_here(1, 3),
                10: lambda: on_c(Gate(1, 2)),
                11: lambda: (on_y(Gate(1, 4)), whole(Gate(1, 0)), begin(gate_loads(1, 0))),
            })
            out_ref[...] = nt(by_all[rows_of(t, b), :], wdv[rows_of(j, FU), :]).astype(BF16)

        pltpu.emit_pipeline(body, grid=(NU, T // b), in_specs=[], out_specs=[pl.BlockSpec((b, FU), lambda j, t: (t, j))])(DH)

    def by_hidden_0():
        b, n = 512, 1152

        def body(gate_ref, up_ref, bg_ref, bu_ref):
            i, j = pl.program_id(0), pl.program_id(1)
            by_hid = nt(by_all[rows_of(i, b), :], wdv[rows_of(j, n), :]).astype(BF16).astype(F32)
            gate, up = gate_ref[...], up_ref[...]
            s = jax.nn.sigmoid(gate)
            silu = gate * s
            bu_ref[...] = (by_hid * silu).astype(BF16)
            bg_ref[...] = (by_hid * up * (s + silu * (1 - s))).astype(BF16)

        deep = pl.BlockSpec((b, n), lambda i, j: (i, j), pipeline_mode=pl.Buffered(3))
        tile = pl.BlockSpec((b, n), lambda i, j: (i, j))
        pltpu.emit_pipeline(body, grid=(T // b, FF // n), in_specs=[deep, deep], out_specs=[tile, tile])(
            PRE.at[0], PRE.at[1], DG.at[0, 0], DG.at[0, 1])

    def by_input():
        b = 256

        def body(bg_ref, bu_ref, h_ref):
            rows = rows_of(pl.program_id(0), b)
            by_a = nt(bg_ref[...], wgu[0]).astype(BF16).astype(F32) + nt(bu_ref[...], wgu[1]).astype(BF16).astype(F32)
            by_a = by_a.astype(BF16).astype(F32)
            wide = h_ref[...].astype(F32)
            scale = lax.rsqrt(jnp.mean(wide * wide, -1, keepdims=True) + 1e-6)
            along = jnp.mean(by_a * wide, -1, keepdims=True)
            by_h = by_a * scale - wide * (scale * scale * scale * along)
            by_all[rows, :] = by_all[rows, :] + by_h.astype(BF16)

        row, wide_row = pl.BlockSpec((b, D), lambda i: (i, 0)), pl.BlockSpec((b, FF), lambda i: (i, 0))
        pltpu.emit_pipeline(body, grid=(T // b,), in_specs=[wide_row, wide_row, row], out_specs=[])(DG.at[1, 0], DG.at[1, 1], H1)

    def send_c(i, k, is_d):
        s, q, e = (SCD, RCD, i + 4) if is_d else (SC, RC, i)
        return remote(s.at[i, k], q.at[i, k], c_send.at[e, k], c_recv.at[e, k], to_c)

    def send_x(i, is_d):
        s, q, e = (SXD, RXD, i + 4) if is_d else (SX, RX, i)
        return remote(s.at[i], q.at[i], x_send.at[e], x_recv.at[e], to_x)

    def grad_gu(layer, m):
        i = 2 * layer + m

        def scoped(lhs):
            b = 768
            by = pl.BlockSpec((T, b), lambda j: (0, j))
            both = pl.BlockSpec((2, BG, b), lambda j: (0, 0, j))
            single = pl.BlockSpec((BG, b), lambda j: (0, j))

            def rows(one, two):
                return [
                    pltpu.make_async_copy(AT.at[layer, pl.ds(one * BG, BG), :], lhs.at[pl.ds(0, BG), :], load_sem.at[0, 0]),
                    pltpu.make_async_copy(AT.at[layer, pl.ds(two * BG, BG), :], lhs.at[pl.ds(BG, BG), :], load_sem.at[0, 1]),
                ]

            first, second = rows(dxc, dc), rows(dx_, d)
            begin(first)

            def body_c(by_ref, out_ref):
                pl.when(pl.program_id(0) == 0)(lambda: end(first))
                g = nn(lhs[...], by_ref[...]).astype(BF16)
                out_ref[0] = g[:BG]
                out_ref[1] = g[BG:]

            pltpu.emit_pipeline(body_c, grid=(FF // b,), in_specs=[by], out_specs=[both])(DG.at[layer, m], SC.at[i])
            begin(second)
            send_c(i, 0, False).start()
            send_c(i, 1, False).start()
            send_c(i, 0, False).wait_recv()

            def body_x(by_ref, came_ref, x_ref, own_ref):
                pl.when(pl.program_id(0) == 0)(lambda: end(second))
                g = nn(lhs[...], by_ref[...]).astype(BF16)
                x_ref[...] = (g[:BG].astype(F32) + came_ref[...].astype(F32)).astype(BF16)
                own_ref[...] = g[BG:]

            pltpu.emit_pipeline(body_x, grid=(FF // b,), in_specs=[by, single], out_specs=[single, single])(
                DG.at[layer, m], RC.at[i, 0], SX.at[i], OWN.at[i])
            send_x(i, False).start()

        pl.run_scoped(scoped, pltpu.VMEM((2 * BG, T), BF16))

    def grad_d(layer):
        b = 384
        n = BD // b
        row = pl.BlockSpec((b, D), lambda j: (j, 0))

        def hid_of(block):
            return pl.BlockSpec((T, b), lambda j: (0, block * n + j))

        def body(hid_ref, out_ref):
            out_ref[...] = tn(hid_ref[...], by_all[...]).astype(BF16)

        def body_x(hid_ref, came_ref, out_ref):
            g = tn(hid_ref[...], by_all[...]).astype(BF16)
            out_ref[...] = (g.astype(F32) + came_ref[...].astype(F32)).astype(BF16)

        def to_core(k, _):
            block = 2 * ((1 - xx) * (1 - k) + xx * k) + 1 - cc
            pltpu.emit_pipeline(body, grid=(n,), in_specs=[hid_of(block)], out_specs=[row])(HID.at[layer], SCD.at[layer, k])
            send_c(layer, k, True).start()
            return 0

        lax.fori_loop(0, 2, to_core, 0)
        send_c(layer, 0, True).wait_recv()
        pltpu.emit_pipeline(body_x, grid=(n,), in_specs=[hid_of(dx_), row], out_specs=[row])(HID.at[layer], RCD.at[layer, 0], SXD.at[layer])
        send_x(layer, True).start()
        pltpu.emit_pipeline(body, grid=(n,), in_specs=[hid_of(d)], out_specs=[row])(HID.at[layer], OWND.at[layer])

    def finish(i, is_d):
        send_x(i, is_d).wait_recv()
        send_c(i, 1, is_d).wait_recv()
        rows, cols, b, total = (BD, D, 384, tot_d) if is_d else (BG, FF, 96, tot_g)

        def body(own_ref, core_ref, came_ref, out_ref):
            g = (own_ref[...].astype(F32) + core_ref[...].astype(F32) + came_ref[...].astype(F32)).astype(BF16)
            out_ref[...] = g
            g = g.astype(F32)
            total[...] += jnp.sum((g * g).reshape(b // 8, 8, cols), axis=0)

        row = pl.BlockSpec((b, cols), lambda j: (j, 0))
        pipe = pltpu.emit_pipeline(body, grid=(rows // b,), in_specs=[row] * 3, out_specs=[row])
        if is_d:
            pipe(OWND.at[i], RCD.at[i, 1], RXD.at[i], gd.at[i])
        else:
            layer, m = i // 2, i % 2
            pl.when(m == 0)(lambda: pipe(OWN.at[i], RC.at[i, 1], RX.at[i], gg.at[layer]))
            pl.when(m == 1)(lambda: pipe(OWN.at[i], RC.at[i, 1], RX.at[i], gu.at[layer]))

    norm()
    on_y(Gate(0, 0))
    on_y(Gate(0, 1))
    on_c(Gate(0, 0))
    gate_up(0)
    on_c(Down(0, 0))
    on_y(Down(0, 1))
    on_c(Down(0, 1))
    on_y(Down(1, 0))
    whole(Down(0, 0))
    whole(Down(0, 1))
    begin(down_loads(0))
    end(down_loads(0))
    down()
    pltpu.make_async_copy(dy, by_all, by_sem).wait()
    whole(Down(1, 0))
    whole(Down(1, 1))
    begin(down_loads(1))
    by_hidden_1()
    gate_up(1)

    def backward(i, _):
        layer = 1 - i
        pl.when(i == 0)(lambda: begin(down_loads(0)))
        grad_d(layer)

        @pl.when(i == 1)
        def _():
            end(down_loads(0))
            by_hidden_0()

        def both(m, _):
            grad_gu(layer, m)
            return 0

        lax.fori_loop(0, 2, both, 0)
        pl.when(i == 0)(by_input)
        return 0

    lax.fori_loop(0, L, backward, 0)
    tot_g[...] = jnp.zeros_like(tot_g)
    tot_d[...] = jnp.zeros_like(tot_d)

    def finish_layer(n, _):
        layer = 1 - n
        finish(layer, True)

        def both(m, _):
            finish(2 * layer + m, False)
            return 0

        return lax.fori_loop(0, 2, both, 0)

    lax.fori_loop(0, L, finish_layer, 0)

    mine = tot_d[:, pl.ds(0, 128)]
    for n in range(1, D // 128):
        mine = mine + tot_d[:, pl.ds(n * 128, 128)]
    for n in range(FF // 128):
        mine = mine + tot_g[:, pl.ds(n * 128, 128)]
    sq_all[d] = mine
    exchange = [remote(sq_all.at[d], sq_all.at[d], sq_send.at[n], sq_recv.at[n], to) for n, to in enumerate((to_c, to_x, to_xc))]
    begin(exchange)
    for c in exchange:
        c.wait_recv()
    sq[...] = ((sq_all[0] + sq_all[1]) + sq_all[2]) + sq_all[3]
    for c in exchange:
        c.wait_send()

    for unit in every:
        for hop in range(4):
            for c in unit.copies(hop):
                c.wait_send()

    def sent(layer, _):
        for i, is_d in ((2 * layer, False), (2 * layer + 1, False), (layer, True)):
            send_c(i, 0, is_d).wait_send()
            send_c(i, 1, is_d).wait_send()
            send_x(i, is_d).wait_send()
        return 0

    lax.fori_loop(0, L, sent, 0)


def fused(x, dy, wg, wu, wd):
    def hbm(*shape, dtype=BF16):
        return jax.ShapeDtypeStruct(shape, dtype)

    outs = [
        hbm(L, BG, FF), hbm(L, BG, FF), hbm(L, BD, D), hbm(8, 128, dtype=F32),
        hbm(L, 2, D, FF), hbm(L, FF, D), hbm(L, D, T), hbm(T, D), hbm(L, T, FF), hbm(2, T, FF, dtype=F32), hbm(T, FF), hbm(L, 2, T, FF),
        hbm(4, 2, BG, FF), hbm(4, 2, BG, FF), hbm(4, BG, FF), hbm(4, BG, FF), hbm(4, BG, FF),
        hbm(2, 2, BD, D), hbm(2, 2, BD, D), hbm(2, BD, D), hbm(2, BD, D), hbm(2, BD, D),
    ]
    specs = [ANY] * len(outs)
    specs[3] = pl.BlockSpec(memory_space=pltpu.VMEM)
    dma = pltpu.SemaphoreType.DMA
    return pl.pallas_call(
        mega,
        out_shape=outs,
        in_specs=[ANY] * 5,
        out_specs=specs,
        scratch_shapes=[
            pltpu.VMEM((2, D, FF), BF16), pltpu.VMEM((FF, D), BF16), pltpu.VMEM((T, D), BF16), pltpu.VMEM((T, D), BF16),
            pltpu.VMEM((8, FF), F32), pltpu.VMEM((8, D), F32), pltpu.VMEM((4, 8, 128), F32),
            dma((L, NU, 2, 4)), dma((L, NU, 2, 4)), dma((L, 2, 4)), dma((L, 2, 4)), dma((6, 2)), dma((6, 2)), dma((6,)), dma((6,)),
            dma((3,)), dma((3,)), dma((2, 4)), dma((4,)), dma,
        ],
        compiler_params=pltpu.CompilerParams(collective_id=0, has_side_effects=True, vmem_limit_bytes=67043328),
        name="step",
    )(x, dy, wg, wu, wd)[:4]


def adamw(w, m, v, g):
    m = 0.9 * m + 0.1 * g
    v = 0.95 * v + 0.05 * g * g
    step = m * lax.rsqrt(v + 1e-8) + 0.1 * w
    return (w - 0.02 * step).astype(BF16), m, v


def solution(mesh):
    def step(x, dy, *arrays):
        weights, m, v = (arrays[i : i + 3] for i in (0, 3, 6))
        *gradients, sq = fused(x[0], dy[0], *weights)
        squares = jnp.sum(sq)
        count = lax.psum(1, "dp") * sum(g.size for g in gradients)
        factor = jnp.minimum(1.0, 0.5 * lax.rsqrt(squares / count + 1e-30))
        new = [adamw(w.astype(F32), m, v, g.astype(F32) * factor) for w, m, v, g in zip(weights, m, v, gradients, strict=True)]
        return tuple(one[which] for which in range(3) for one in new)

    states, cut = P(("rep", "dp"), None, None), P(None, "dp", None)
    return jax.shard_map(
        step,
        mesh=mesh,
        in_specs=(states, states) + (cut,) * 9,
        out_specs=(P("rep", "dp", None),) * 9,
        check_vma=False,
    )
```

time: 1170 us -> 730 us (0.62)
  Pallas kernels: 0 us -> 665 us
  matrix products: 531 us -> 0 us
  waiting for transfers between devices: 491 us -> 0 us
  local copies, waits for them, and re-layouts: 31.9 us -> 0 us
  other arithmetic: 88.6 us -> 63 us
  between operations: 17.5 us -> 1.52 us
    pallas_call x0 -> x1, Pallas kernels: none -> 665 us  [fused(): pl.pallas_call(mega, out_shape=outs, in_specs=[ANY] * 5, out_specs=specs,...]
    dot_general x15 -> x0, matrix products: 531 us -> none  [the longest x5 185 us: layer(): up = jnp.dot(a, w['w_up'], preferred_element_type=jnp.float32)]
    reduce_scatter x6 -> x0, waiting for transfers between devices: 266 us -> none  [step(): lax.psum_scatter(by_w[name], 'dp', scatter_dimension=0, tiled=True)]
    all_gather x6 -> x0, waiting for transfers between devices: 224 us -> none  [fetched(): lax.all_gather(w[number], 'dp', axis=0, tiled=True)]
    reduce_sum x4 -> x1, other arithmetic: 21.1 us -> 1.27 us  [step(): squares = jnp.sum(sq)]
    unnamed x18 -> x0, local copies, waits for them, and re-layouts: 16.1 us -> none
    slice x3 -> x0, local copies, waits for them, and re-layouts: 15.9 us -> none  [fetched(): w[number]]
  transfers between devices with their start and end apart: 12 -> 0, of which waited for: 10 -> 0; matrix products, arithmetic and copies ran while one was open for 36% -> 0% of each run, Pallas kernels for 0% -> 0%
where the time goes in v2:
time: 730 us; the launch traced here: 729 us
  Pallas kernels  665 us (91%)
  other arithmetic  63 us (9%)
    pallas_call x1, Pallas kernels, fused(): pl.pallas_call(mega, out_shape=outs, in_specs=[ANY] * 5, out_specs=specs,...  665 us
    convert_element_type x2, other arithmetic, adamw(): return ((w - 0.02 * step).astype(BF16), m, v)  61.7 us

profile of v2, /device:TPU:0, one launch (start us, length us, event | category | flops | bytes accessed | tf_op | source)
XLA Modules:
  0.0 729.1 jit_solution(9333998969114144144)
XLA Ops:
  0.6 664.5 %step.1 = (bf16[2,288,4608]{2,1,0:T(8,128)(2,1)}, bf16[2,288,4608]{2,1,0:T(8,128)(2,1)}, bf16[2,1152,1152]{2,1,0:T(8,128)(2,1)}, f32[8,128]{1,0:T(8,128)}, bf16[...) custom-call(bf16[2048,1152]{1,0:T(8,128)(2,1)} %bitcast.2, ...), custom_call_target="tpu_custom_call" | custom-call | tf_op jit(solution)/shard_map/step/pallas_call | solution.py:479
  665.2 1.3 reduce_sum.9
  667.1 22.1 %fusion.8 = (bf16[2,1152,1152]{2,1,0:T(8,128)(2,1)}, f32[2,1152,1152]{2,1,0:T(8,128)}, f32[2,1152,1152]{2,1,0:T(8,128)}) fusion(bf16[2,1152,1152]{2,1,0:T(8,128)(2,1)} %wd.1, f32[]{:T(128)S(6)} %min_shard_map.3, bf16[2,1152,1152]{2,1,0:T(8,128)(2,1)} %get-tuple-element.16, f32[2,1152,1152]{2,1,0:T(8,128)} %param.21, f32[2,1152,1152]{2,1,0:T(8,128)} %param.18), kind=kLoop, calls=%fused_computation.17 | loop fusion | flops 45121536 | bytes 58392580 | tf_op jit(solution)/shard_map/convert_element_type | solution.py:499
  689.3 39.6 %fusion.2 = (bf16[2,288,4608]{2,1,0:T(8,128)(2,1)}, f32[2,288,4608]{2,1,0:T(8,128)}, f32[2,288,4608]{2,1,0:T(8,128)}, bf16[2,288,4608]{2,1,0:T(8,128)(2,1)}, f32...) fusion(bf16[2,288,4608]{2,1,0:T(8,128)(2,1)} %wg.1, f32[]{:T(128)S(6)} %min_shard_map.3, ...), kind=kLoop, calls=%fused_computation.11 | loop fusion | flops 90243072 | bytes 116785152 | tf_op jit(solution)/shard_map/convert_element_type | solution.py:499

commit v3 on v2

v3 whole, which is shorter than its diff:
```python
import jax
import jax.numpy as jnp
from jax import lax
from jax.experimental import pallas as pl
from jax.experimental.pallas import tpu as pltpu
from jax.sharding import PartitionSpec as P

MESH = pl.DeviceIdType.MESH
T, D, FF, L = 2048, 1152, 4608, 2
BG, BD = D // 4, FF // 4
FU = 768
NU = FF // FU
ND = 4
F32, BF16 = jnp.float32, jnp.bfloat16
ANY = pl.BlockSpec(memory_space=pl.ANY)


def nn(a, b):
    return lax.dot_general(a, b, (((1,), (0,)), ((), ())), preferred_element_type=F32)


def nt(a, b):
    return lax.dot_general(a, b, (((1,), (1,)), ((), ())), preferred_element_type=F32)


def tn(a, b):
    return lax.dot_general(a, b, (((0,), (0,)), ((), ())), preferred_element_type=F32)


def mega(x, dy, wg, wu, wd, *refs):
    (gg, gu, gd, sq, GU, WD, AT, H1, HID, PRE, DG, SG, RG, SD, RD) = refs[:15]
    (wgu, wdv, acts, tot_g, tot_d, sq_all) = refs[15:21]
    (gs, gr, ds_, dr, gcs, gcr, gxs, gxr, dcs, dcr, dxs, dxr, sq_send, sq_recv, load_sem, wd_sem, by_sem) = refs[21:]
    a_all = acts.at[0]
    r, d = lax.axis_index("rep"), lax.axis_index("dp")
    xx, cc = d // 2, d % 2
    dc, dx_, dxc = 2 * xx + 1 - cc, 2 * (1 - xx) + cc, 2 * (1 - xx) + 1 - cc
    to_c, to_x, to_xc, to_y = (r, dc), (r, dx_), (r, dxc), (1 - r, d)

    barrier = pltpu.get_barrier_semaphore()
    for to in (to_c, to_x, to_xc, to_y):
        pl.semaphore_signal(barrier, inc=1, device_id=to, device_id_type=MESH)
    pl.semaphore_wait(barrier, 4)

    def remote(src, dst, s, q, to):
        return pltpu.make_async_remote_copy(src_ref=src, dst_ref=dst, send_sem=s, recv_sem=q, device_id=to, device_id_type=MESH)

    def piece(arg, full, layer, block, r0, rows, cols, s, q, hop):
        half = rows // 2
        if hop == 0:
            mine = r0 + r * half
            return remote(arg.at[layer, pl.ds(mine, half), cols], full.at[pl.ds(d * block + mine, half), cols], s, q, to_x)
        if hop == 1:
            at = full.at[pl.ds(dx_ * block + r0 + r * half, half), cols]
            return remote(at, at, s, q, to_y)
        if hop == 2:
            return remote(arg.at[layer, pl.ds(r0, rows), cols], full.at[pl.ds(d * block + r0, rows), cols], s, q, to_c)
        at = full.at[pl.ds(dx_ * block + r0, rows), cols]
        return remote(at, at, s, q, to_c)

    def columns(u):
        return pl.ds(u * FU if isinstance(u, int) else pl.multiple_of(u * FU, FU), FU)

    class Gate:
        def __init__(self, layer, u):
            self.layer, self.u = layer, u

        def copies(self, hop):
            layer, u = self.layer, self.u
            return [piece(arg, GU.at[layer, m], layer, BG, 0, BG, columns(u), gs.at[layer, u, m, hop], gr.at[layer, u, m, hop], hop)
                    for m, arg in enumerate((wg, wu))]

    class Down:
        def __init__(self, layer, u):
            self.layer, self.u = layer, u

        def copies(self, hop):
            layer, u = self.layer, self.u
            return [piece(wd, WD.at[layer], layer, BD, u * (BD // ND), BD // ND, pl.ds(0, D), ds_.at[layer, u, hop], dr.at[layer, u, hop], hop)]

    def start(unit, hop):
        for c in unit.copies(hop):
            c.start()

    def arrive(unit, hop):
        for c in unit.copies(hop):
            c.wait_recv()

    def on_y(unit):
        arrive(unit, 0)
        start(unit, 1)

    def on_c(unit):
        arrive(unit, 1)
        start(unit, 3)

    def whole(unit):
        arrive(unit, 2)
        arrive(unit, 3)

    every = [unit(layer, u) for layer in range(L) for unit, n in ((Gate, NU), (Down, ND)) for u in range(n)]
    for unit in every:
        start(unit, 0)
    for unit in every:
        start(unit, 2)
    pltpu.make_async_copy(dy, acts.at[1], by_sem).start()

    def gate_loads(layer, u):
        out = []
        for m, arg in enumerate((wg, wu)):
            for i, b in enumerate((d, dc, dx_, dxc)):
                rows = pl.ds(b * BG, BG)
                src = GU.at[layer, m, rows, columns(u)] if i else arg.at[layer, :, columns(u)]
                out.append(pltpu.make_async_copy(src, wgu.at[m, rows, columns(u)], load_sem.at[m, i]))
        return out

    def down_loads(layer, u):
        out = []
        for i, b in enumerate((d, dc, dx_, dxc)):
            part = pl.ds(u * (BD // ND), BD // ND)
            rows = pl.ds(b * BD + u * (BD // ND), BD // ND)
            out.append(pltpu.make_async_copy(WD.at[layer, rows, :] if i else wd.at[layer, part, :], wdv.at[rows, :], wd_sem.at[i, u]))
        return out

    def all_down_loads(layer):
        return [c for u in range(ND) for c in down_loads(layer, u)]

    def begin(copies):
        for c in copies:
            c.start()

    def end(copies):
        for c in copies:
            c.wait()

    def begin_when(cases):
        for when, c in cases:
            if when is True:
                c.start()
            else:
                pl.when(when)(c.start)

    def end_when(cases):
        for when, c in cases:
            if when is True:
                c.wait()
            else:
                pl.when(when)(c.wait)

    def norm_of(h):
        wide = h.astype(F32)
        scale = lax.rsqrt(jnp.mean(wide * wide, -1, keepdims=True) + 1e-6)
        return wide * scale

    def rows_of(i, b):
        return pl.ds(pl.multiple_of(i * b, b), b)

    def at_steps(step, hooks):
        for when, what in hooks.items():

            @pl.when(step == when)
            def _(what=what):
                what()

    def norm():
        b = 512

        def body(x_ref, at_ref):
            a = norm_of(x_ref[...])
            a_all[rows_of(pl.program_id(0), b), :] = a.astype(BF16)
            at_ref[...] = a.T.astype(BF16)

        pltpu.emit_pipeline(
            body, grid=(T // b,), in_specs=[pl.BlockSpec((b, D), lambda i: (i, 0))], out_specs=[pl.BlockSpec((D, b), lambda i: (0, i))],
        )(x, AT.at[0])

    def gate_up(layer, hooks):
        b = 1024

        def body(gate_ref, up_ref, hid_ref):
            u, t = pl.program_id(0), pl.program_id(1)
            pl.when(t == 0)(lambda: end(gate_loads(layer, u)))
            at_steps(2 * u + t, hooks)
            a = a_all[rows_of(t, b), :]

            @pl.when((t == 1) & (u + 1 < NU))
            def _():
                whole(Gate(layer, u + 1))
                begin(gate_loads(layer, u + 1))

            gate = nn(a, wgu[0, :, columns(u)])
            gate_ref[...] = gate
            up = nn(a, wgu[1, :, columns(u)])
            up_ref[...] = up
            hid_ref[...] = (gate * jax.nn.sigmoid(gate) * up).astype(BF16)

        tile = pl.BlockSpec((b, FU), lambda u, t: (t, u))
        pltpu.emit_pipeline(body, grid=(NU, T // b), in_specs=[], out_specs=[tile] * 3)(PRE.at[layer, 0], PRE.at[layer, 1], HID.at[layer])

    def down():
        b = 256

        def body(x_ref, hid_ref, h_ref, at_ref):
            i = pl.program_id(0)
            at_steps(i, {
                2: lambda: on_y(Gate(1, 1)),
                3: lambda: on_c(Gate(1, 0)),
                5: lambda: (on_y(Gate(1, 2)), on_c(Gate(1, 1))),
                7: lambda: (on_y(Gate(1, 3)), whole(Gate(1, 0)), begin(gate_loads(1, 0))),
            })
            h = x_ref[...] + nn(hid_ref[...], wdv[...]).astype(BF16)
            h_ref[...] = h
            a = norm_of(h)
            a_all[rows_of(i, b), :] = a.astype(BF16)
            at_ref[...] = a.T.astype(BF16)

        row = pl.BlockSpec((b, D), lambda i: (i, 0))
        pltpu.emit_pipeline(
            body, grid=(T // b,), in_specs=[row, pl.BlockSpec((b, FF), lambda i: (i, 0))],
            out_specs=[row, pl.BlockSpec((D, b), lambda i: (0, i))],
        )(x, HID.at[0], H1, AT.at[1])

    def by_hidden(layer):
        b, n = 512, 1152

        def body(gate_ref, up_ref, bg_ref, bu_ref):
            i, j = pl.program_id(0), pl.program_id(1)
            by_hid = nt(acts[layer, rows_of(i, b), :], wdv[rows_of(j, n), :]).astype(BF16).astype(F32)
            gate, up = gate_ref[...], up_ref[...]
            s = jax.nn.sigmoid(gate)
            silu = gate * s
            bu_ref[...] = (by_hid * silu).astype(BF16)
            bg_ref[...] = (by_hid * up * (s + silu * (1 - s))).astype(BF16)

        deep = pl.BlockSpec((b, n), lambda i, j: (i, j), pipeline_mode=pl.Buffered(3))
        tile = pl.BlockSpec((b, n), lambda i, j: (i, j))
        pltpu.emit_pipeline(body, grid=(T // b, FF // n), in_specs=[deep, deep], out_specs=[tile, tile])(
            PRE.at[layer, 0], PRE.at[layer, 1], DG.at[layer, 0], DG.at[layer, 1])

    def by_input():
        b = 256

        def body(bg_ref, bu_ref, h_ref):
            rows = rows_of(pl.program_id(0), b)
            by_a = nt(bg_ref[...], wgu[0]).astype(BF16).astype(F32) + nt(bu_ref[...], wgu[1]).astype(BF16).astype(F32)
            by_a = by_a.astype(BF16).astype(F32)
            wide = h_ref[...].astype(F32)
            scale = lax.rsqrt(jnp.mean(wide * wide, -1, keepdims=True) + 1e-6)
            along = jnp.mean(by_a * wide, -1, keepdims=True)
            by_h = by_a * scale - wide * (scale * scale * scale * along)
            acts[0, rows, :] = acts[1, rows, :] + by_h.astype(BF16)

        row, wide_row = pl.BlockSpec((b, D), lambda i: (i, 0)), pl.BlockSpec((b, FF), lambda i: (i, 0))
        pltpu.emit_pipeline(body, grid=(T // b,), in_specs=[wide_row, wide_row, row], out_specs=[])(DG.at[1, 0], DG.at[1, 1], H1)

    def block_of(k):
        return 2 * ((1 - xx) * (1 - k // 2) + xx * (k // 2)) + (1 - cc) * (1 - k % 2) + cc * (k % 2)

    BT, BC = 384, 768
    DT, GT = BD // BT, FF // BC

    def d_rows(j):
        return pl.ds(pl.multiple_of(j * BT, BT), BT)

    def d_core(layer, p, j):
        at = (layer, 2 * p, d_rows(j), slice(None))
        return remote(SD.at[at], RD.at[at], dcs.at[layer, p, j], dcr.at[layer, p, j], to_c)

    def d_x(layer, j):
        at = (layer, 1, d_rows(j), slice(None))
        return remote(SD.at[at], RD.at[at], dxs.at[layer, j], dxr.at[layer, j], to_x)

    def g_cols(j):
        return pl.ds(pl.multiple_of(j * BC, BC), BC)

    def g_core(i, p, j):
        at = (i, 2 * p, slice(None), g_cols(j))
        return remote(SG.at[at], RG.at[at], gcs.at[i, p, j], gcr.at[i, p, j], to_c)

    def g_x(i, j):
        at = (i, 1, slice(None), g_cols(j))
        return remote(SG.at[at], RG.at[at], gxs.at[i, j], gxr.at[i, j], to_x)

    def square(total, g, cols):
        g = g.astype(F32)
        total[...] += jnp.sum((g * g).reshape(g.shape[0] // 8, 8, cols), axis=0)

    def grad_d(layer, p):
        def scoped(made, came, made_sem, came_sem):
            def to_hbm(n):
                def copy(dst):
                    return pltpu.make_async_copy(made.at[n % 2], dst, made_sem.at[n % 2])

                stage = copy(SD.at[layer, 2 * p + n // DT * (1 - p), d_rows(n % DT), :])
                return [(n < DT, stage), (n >= DT, copy(gd.at[layer, d_rows(n % DT), :]))] if p else [(True, stage)]

            def from_hbm(j, k):
                src = RD.at[layer, 1 if k else 2 * p, d_rows(j), :]
                return pltpu.make_async_copy(src, came.at[j % 2, k], came_sem.at[j % 2, k])

            def fetch(j):
                d_core(layer, p, j).wait_recv()
                from_hbm(j, 0).start()
                if p:
                    d_x(layer, j).wait_recv()
                    from_hbm(j, 1).start()

            def send(n):
                end_when(to_hbm(n))
                pl.when(n < DT)(lambda: d_core(layer, p, n % DT).start())
                if p == 0:
                    pl.when(n >= DT)(lambda: d_x(layer, n % DT).start())

            def body(hid_ref):
                n = pl.program_id(0)
                if p == 0:
                    pl.when((layer == 1) & (n == 3))(lambda: on_c(Down(1, 3)))

                    @pl.when((layer == 1) & (n == 5))
                    def _():
                        for u in range(ND):
                            whole(Down(1, u))
                        begin(all_down_loads(1))

                made[n % 2] = tn(hid_ref[...], acts[layer]).astype(BF16)

                @pl.when(n >= DT)
                def _():
                    j = n % DT
                    from_hbm(j, 0).wait()
                    g = made[n % 2].astype(F32) + came[j % 2, 0].astype(F32)
                    if p:
                        from_hbm(j, 1).wait()
                        g = g + came[j % 2, 1].astype(F32)
                    g = g.astype(BF16)
                    made[n % 2] = g
                    if p:
                        square(tot_d, g, D)

                begin_when(to_hbm(n))
                pl.when(n > 0)(lambda: send(n - 1))
                pl.when((n >= DT - 1) & (n < 2 * DT - 1))(lambda: fetch(n - (DT - 1)))

            hid = pl.BlockSpec((T, BT), lambda n: (0, block_of(2 * p + n // DT) * DT + n % DT))
            pltpu.emit_pipeline(body, grid=(2 * DT,), in_specs=[hid], out_specs=[])(HID.at[layer])
            send(2 * DT - 1)

        dma = pltpu.SemaphoreType.DMA
        pl.run_scoped(scoped, pltpu.VMEM((2, BT, D), BF16), pltpu.VMEM((2, 1 + p, BT, D), BF16), dma((2,)), dma((2, 2)))

    def grad_gu(layer, p):
        steps = 2 * GT

        def scoped(lhs, made, came, made_sem, own_sem, came_sem):
            rows = [
                pltpu.make_async_copy(AT.at[layer, pl.ds(block_of(2 * p + h) * BG, BG), :], lhs.at[pl.ds(h * BG, BG), :], load_sem.at[0, h])
                for h in range(2)
            ]

            def to_hbm(q, h):
                m, cols = q // GT, g_cols(q % GT)

                def copy(dst):
                    return pltpu.make_async_copy(made.at[q % 4, h], dst, (made_sem, own_sem)[h].at[q % 4])

                if p and h:
                    return [(m == 0, copy(gg.at[layer, :, cols])), (m == 1, copy(gu.at[layer, :, cols]))]
                return [(True, copy(SG.at[2 * layer + m, 2 * p + h, :, cols]))]

            def from_hbm(q, k):
                src = RG.at[2 * layer + q // GT, 1 if k else 2 * p, :, g_cols(q % GT)]
                return pltpu.make_async_copy(src, came.at[q % 2, k], came_sem.at[q % 2, k])

            def stage_1(q):
                end_when(to_hbm(q, 0))
                g_core(2 * layer + q // GT, p, q % GT).start()

            def stage_2(q):
                i, j = 2 * layer + q // GT, q % GT
                g_core(i, p, j).wait_recv()
                from_hbm(q, 0).start()
                if p:
                    g_x(i, j).wait_recv()
                    from_hbm(q, 1).start()

            def stage_3(q):
                from_hbm(q, 0).wait()
                g = made[q % 4, 1].astype(F32) + came[q % 2, 0].astype(F32)
                if p:
                    from_hbm(q, 1).wait()
                    g = g + came[q % 2, 1].astype(F32)
                g = g.astype(BF16)
                made[q % 4, 1] = g
                if p:
                    square(tot_g, g, BC)
                begin_when(to_hbm(q, 1))

            def stage_4(q):
                end_when(to_hbm(q, 1))
                if p == 0:
                    g_x(2 * layer + q // GT, q % GT).start()

            def stage(q, late):
                what = (stage_1, stage_2, stage_3, stage_4)[late - 1]
                pl.when((q >= late) & (q < steps + late))(lambda: what(q - late))

            begin(rows)

            def body(by_ref):
                q = GT * pl.program_id(0) + pl.program_id(1)
                pl.when(q == 0)(lambda: end(rows))
                stage(q, 4)
                g = nn(lhs[...], by_ref[0]).astype(BF16)
                made[q % 4, 0] = g[:BG]
                made[q % 4, 1] = g[BG:]
                for late in (3, 2, 1):
                    stage(q, late)
                begin_when(to_hbm(q, 0))

            by = pl.BlockSpec((1, T, BC), lambda m, n: (m, 0, n))
            pltpu.emit_pipeline(body, grid=(2, GT), in_specs=[by], out_specs=[])(DG.at[layer])

            def drain(n, _):
                for late in (4, 3, 2, 1):
                    stage(steps + n, late)
                return 0

            lax.fori_loop(0, 4, drain, 0)

        four, two = pltpu.SemaphoreType.DMA((4,)), pltpu.SemaphoreType.DMA((2, 2))
        pl.run_scoped(
            scoped, pltpu.VMEM((2 * BG, T), BF16), pltpu.VMEM((4, 2, BG, BC), BF16), pltpu.VMEM((2, 1 + p, BG, BC), BF16), four, four, two)

    norm()
    on_y(Gate(0, 0))
    on_y(Gate(0, 1))
    on_c(Gate(0, 0))
    whole(Gate(0, 0))
    begin(gate_loads(0, 0))
    hooks = {2 * u: lambda u=u: (on_y(Gate(0, u + 2)), on_c(Gate(0, u + 1))) for u in range(NU - 2)}
    hooks |= {
        7: lambda: on_y(Down(0, 0)),
        8: lambda: (on_y(Down(0, 1)), on_c(Gate(0, 5))),
        9: lambda: (on_y(Down(0, 2)), on_c(Down(0, 0))),
        10: lambda: (on_y(Down(0, 3)), on_c(Down(0, 1))),
        11: lambda: on_c(Down(0, 2)),
    }
    gate_up(0, hooks)
    whole(Down(0, 0))
    begin(down_loads(0, 0))
    whole(Down(0, 1))
    begin(down_loads(0, 1))
    whole(Down(0, 2))
    begin(down_loads(0, 2))
    on_c(Down(0, 3))
    on_y(Gate(1, 0))
    whole(Down(0, 3))
    begin(down_loads(0, 3))
    end(all_down_loads(0))
    down()
    hooks = {
        0: lambda: on_c(Gate(1, 2)),
        1: lambda: on_y(Gate(1, 4)),
        2: lambda: on_c(Gate(1, 3)),
        3: lambda: on_y(Gate(1, 5)),
        4: lambda: on_c(Gate(1, 4)),
        5: lambda: on_y(Down(1, 0)),
        6: lambda: on_c(Gate(1, 5)),
        7: lambda: (on_y(Down(1, 1)), on_c(Down(1, 0))),
        9: lambda: (on_y(Down(1, 2)), on_c(Down(1, 1))),
        11: lambda: (on_y(Down(1, 3)), on_c(Down(1, 2))),
    }
    gate_up(1, hooks)
    pltpu.make_async_copy(dy, acts.at[1], by_sem).wait()

    def backward(i, _):
        layer = 1 - i
        grad_d(layer, 0)
        end(all_down_loads(layer))
        by_hidden(layer)
        pl.when(i == 0)(lambda: begin(all_down_loads(0)))
        grad_gu(layer, 0)
        pl.when(i == 0)(by_input)
        return 0

    lax.fori_loop(0, L, backward, 0)

    tot_g[...] = jnp.zeros_like(tot_g)
    tot_d[...] = jnp.zeros_like(tot_d)

    def rest(i, _):
        grad_d(1 - i, 1)
        grad_gu(1 - i, 1)
        return 0

    lax.fori_loop(0, L, rest, 0)
    mine = tot_d[:, pl.ds(0, 128)]
    for n in range(1, D // 128):
        mine = mine + tot_d[:, pl.ds(n * 128, 128)]
    for n in range(BC // 128):
        mine = mine + tot_g[:, pl.ds(n * 128, 128)]
    sq_all[d] = mine
    exchange = [remote(sq_all.at[d], sq_all.at[d], sq_send.at[n], sq_recv.at[n], to) for n, to in enumerate((to_c, to_x, to_xc))]
    begin(exchange)
    for c in exchange:
        c.wait_recv()
    sq[...] = ((sq_all[0] + sq_all[1]) + sq_all[2]) + sq_all[3]
    for c in exchange:
        c.wait_send()

    for unit in every:
        for hop in range(4):
            for c in unit.copies(hop):
                c.wait_send()

    def sent(layer, _):
        for j in range(DT):
            for c in (d_core(layer, 0, j), d_core(layer, 1, j), d_x(layer, j)):
                c.wait_send()
        for m in range(2):
            for j in range(GT):
                g_core(2 * layer + m, 0, j).wait_send()
                g_core(2 * layer + m, 1, j).wait_send()
                g_x(2 * layer + m, j).wait_send()
        return 0

    lax.fori_loop(0, L, sent, 0)


def fused(x, dy, wg, wu, wd):
    def hbm(*shape, dtype=BF16):
        return jax.ShapeDtypeStruct(shape, dtype)

    outs = [
        hbm(L, BG, FF), hbm(L, BG, FF), hbm(L, BD, D), hbm(8, 128, dtype=F32),
        hbm(L, 2, D, FF), hbm(L, FF, D), hbm(L, D, T), hbm(T, D), hbm(L, T, FF), hbm(L, 2, T, FF, dtype=F32), hbm(L, 2, T, FF),
        hbm(4, 3, BG, FF), hbm(4, 3, BG, FF), hbm(2, 3, BD, D), hbm(2, 3, BD, D),
    ]
    specs = [ANY] * len(outs)
    specs[3] = pl.BlockSpec(memory_space=pltpu.VMEM)
    dma = pltpu.SemaphoreType.DMA
    return pl.pallas_call(
        mega,
        out_shape=outs,
        in_specs=[ANY] * 5,
        out_specs=specs,
        scratch_shapes=[
            pltpu.VMEM((2, D, FF), BF16), pltpu.VMEM((FF, D), BF16), pltpu.VMEM((2, T, D), BF16),
            pltpu.VMEM((8, FU), F32), pltpu.VMEM((8, D), F32), pltpu.VMEM((4, 8, 128), F32),
            dma((L, NU, 2, 4)), dma((L, NU, 2, 4)), dma((L, ND, 4)), dma((L, ND, 4)), dma((4, 2, 6)), dma((4, 2, 6)), dma((4, 6)), dma((4, 6)),
            dma((L, 2, 3)), dma((L, 2, 3)), dma((L, 3)), dma((L, 3)), dma((3,)), dma((3,)), dma((2, 4)), dma((4, ND)), dma,
        ],
        compiler_params=pltpu.CompilerParams(collective_id=0, has_side_effects=True, vmem_limit_bytes=67043328),
        name="step",
    )(x, dy, wg, wu, wd)[:4]


def adamw(w, m, v, g):
    m = 0.9 * m + 0.1 * g
    v = 0.95 * v + 0.05 * g * g
    step = m * lax.rsqrt(v + 1e-8) + 0.1 * w
    return (w - 0.02 * step).astype(BF16), m, v


def solution(mesh):
    def step(x, dy, *arrays):
        weights, m, v = (arrays[i : i + 3] for i in (0, 3, 6))
        *gradients, sq = fused(x[0], dy[0], *weights)
        squares = jnp.sum(sq)
        count = lax.psum(1, "dp") * sum(g.size for g in gradients)
        factor = jnp.minimum(1.0, 0.5 * lax.rsqrt(squares / count + 1e-30))
        new = [adamw(w.astype(F32), m, v, g.astype(F32) * factor) for w, m, v, g in zip(weights, m, v, gradients, strict=True)]
        return tuple(one[which] for which in range(3) for one in new)

    states, cut = P(("rep", "dp"), None, None), P(None, "dp", None)
    return jax.shard_map(
        step,
        mesh=mesh,
        in_specs=(states, states) + (cut,) * 9,
        out_specs=(P("rep", "dp", None),) * 9,
        check_vma=False,
    )
```

time: 730 us -> 644 us (0.88)
  Pallas kernels: 665 us -> 579 us
    pallas_call x1, Pallas kernels: 665 us -> 579 us  [fused(): pl.pallas_call(mega, out_shape=outs, in_specs=[ANY] * 5, out_specs=specs,...]
where the time goes in v3:
time: 644 us; the launch traced here: 643 us
  Pallas kernels  579 us (90%)
  other arithmetic  63 us (10%)
    pallas_call x1, Pallas kernels, fused(): pl.pallas_call(mega, out_shape=outs, in_specs=[ANY] * 5, out_specs=specs,...  579 us
    convert_element_type x2, other arithmetic, adamw(): return ((w - 0.02 * step).astype(BF16), m, v)  61.7 us

profile of v3, /device:TPU:0, one launch (start us, length us, event | category | flops | bytes accessed | tf_op | source)
XLA Modules:
  0.0 643.1 jit_solution(14076696314921043809)
XLA Ops:
  0.6 578.5 %step.1 = (bf16[2,288,4608]{2,1,0:T(8,128)(2,1)}, bf16[2,288,4608]{2,1,0:T(8,128)(2,1)}, bf16[2,1152,1152]{2,1,0:T(8,128)(2,1)}, f32[8,128]{1,0:T(8,128)}, bf16[...) custom-call(bf16[2048,1152]{1,0:T(8,128)(2,1)} %bitcast.2, ...), custom_call_target="tpu_custom_call" | custom-call | tf_op jit(solution)/shard_map/step/pallas_call | solution.py:542
  579.2 1.3 reduce_sum.9
  581.1 22.1 %fusion.8 = (bf16[2,1152,1152]{2,1,0:T(8,128)(2,1)}, f32[2,1152,1152]{2,1,0:T(8,128)}, f32[2,1152,1152]{2,1,0:T(8,128)}) fusion(bf16[2,1152,1152]{2,1,0:T(8,128)(2,1)} %wd.1, f32[]{:T(128)S(6)} %min_shard_map.3, bf16[2,1152,1152]{2,1,0:T(8,128)(2,1)} %get-tuple-element.16, f32[2,1152,1152]{2,1,0:T(8,128)} %param.21, f32[2,1152,1152]{2,1,0:T(8,128)} %param.18), kind=kLoop, calls=%fused_computation.17 | loop fusion | flops 45121536 | bytes 58392580 | tf_op jit(solution)/shard_map/convert_element_type | solution.py:562
  603.3 39.6 %fusion.2 = (bf16[2,288,4608]{2,1,0:T(8,128)(2,1)}, f32[2,288,4608]{2,1,0:T(8,128)}, f32[2,288,4608]{2,1,0:T(8,128)}, bf16[2,288,4608]{2,1,0:T(8,128)(2,1)}, f32...) fusion(bf16[2,288,4608]{2,1,0:T(8,128)(2,1)} %wg.1, f32[]{:T(128)S(6)} %min_shard_map.3, ...), kind=kLoop, calls=%fused_computation.11 | loop fusion | flops 90243072 | bytes 116785152 | tf_op jit(solution)/shard_map/convert_element_type | solution.py:562

commit v4 on v3

--- a/solution.py
+++ b/solution.py
@@ -257,7 +257,7 @@
         return 2 * ((1 - xx) * (1 - k // 2) + xx * (k // 2)) + (1 - cc) * (1 - k % 2) + cc * (k % 2)
 
     BT, BC = 384, 768
-    DT, GT = BD // BT, FF // BC
+    DT, GT, SLOTS = BD // BT, FF // BC, 5
 
     def d_rows(j):
         return pl.ds(pl.multiple_of(j * BT, BT), BT)
@@ -361,7 +361,7 @@
                 m, cols = q // GT, g_cols(q % GT)
 
                 def copy(dst):
-                    return pltpu.make_async_copy(made.at[q % 4, h], dst, (made_sem, own_sem)[h].at[q % 4])
+                    return pltpu.make_async_copy(made.at[q % SLOTS, h], dst, (made_sem, own_sem)[h].at[q % SLOTS])
 
                 if p and h:
                     return [(m == 0, copy(gg.at[layer, :, cols])), (m == 1, copy(gu.at[layer, :, cols]))]
@@ -385,12 +385,12 @@
 
             def stage_3(q):
                 from_hbm(q, 0).wait()
-                g = made[q % 4, 1].astype(F32) + came[q % 2, 0].astype(F32)
+                g = made[q % SLOTS, 1].astype(F32) + came[q % 2, 0].astype(F32)
                 if p:
                     from_hbm(q, 1).wait()
                     g = g + came[q % 2, 1].astype(F32)
                 g = g.astype(BF16)
-                made[q % 4, 1] = g
+                made[q % SLOTS, 1] = g
                 if p:
                     square(tot_g, g, BC)
                 begin_when(to_hbm(q, 1))
@@ -409,11 +409,10 @@
             def body(by_ref):
                 q = GT * pl.program_id(0) + pl.program_id(1)
                 pl.when(q == 0)(lambda: end(rows))
-                stage(q, 4)
                 g = nn(lhs[...], by_ref[0]).astype(BF16)
-                made[q % 4, 0] = g[:BG]
-                made[q % 4, 1] = g[BG:]
-                for late in (3, 2, 1):
+                made[q % SLOTS, 0] = g[:BG]
+                made[q % SLOTS, 1] = g[BG:]
+                for late in (4, 3, 2, 1):
                     stage(q, late)
                 begin_when(to_hbm(q, 0))
 
@@ -427,9 +426,9 @@
 
             lax.fori_loop(0, 4, drain, 0)
 
-        four, two = pltpu.SemaphoreType.DMA((4,)), pltpu.SemaphoreType.DMA((2, 2))
+        five, two = pltpu.SemaphoreType.DMA((SLOTS,)), pltpu.SemaphoreType.DMA((2, 2))
         pl.run_scoped(
-            scoped, pltpu.VMEM((2 * BG, T), BF16), pltpu.VMEM((4, 2, BG, BC), BF16), pltpu.VMEM((2, 1 + p, BG, BC), BF16), four, four, two)
+            scoped, pltpu.VMEM((2 * BG, T), BF16), pltpu.VMEM((SLOTS, 2, BG, BC), BF16), pltpu.VMEM((2, 1 + p, BG, BC), BF16), five, five, two)
 
     norm()
     on_y(Gate(0, 0))
@@ -439,15 +438,17 @@
     begin(gate_loads(0, 0))
     hooks = {2 * u: lambda u=u: (on_y(Gate(0, u + 2)), on_c(Gate(0, u + 1))) for u in range(NU - 2)}
     hooks |= {
-        7: lambda: on_y(Down(0, 0)),
-        8: lambda: (on_y(Down(0, 1)), on_c(Gate(0, 5))),
-        9: lambda: (on_y(Down(0, 2)), on_c(Down(0, 0))),
-        10: lambda: (on_y(Down(0, 3)), on_c(Down(0, 1))),
-        11: lambda: on_c(Down(0, 2)),
+        8: lambda: (on_y(Down(0, 0)), on_c(Gate(0, 5))),
+        9: lambda: on_y(Down(0, 1)),
+        10: lambda: on_c(Down(0, 0)),
+        11: lambda: on_y(Down(0, 2)),
     }
     gate_up(0, hooks)
+    on_c(Down(0, 1))
+    on_y(Down(0, 3))
     whole(Down(0, 0))
     begin(down_loads(0, 0))
+    on_c(Down(0, 2))
     whole(Down(0, 1))
     begin(down_loads(0, 1))
     whole(Down(0, 2))
@@ -562,15 +563,38 @@
     return (w - 0.02 * step).astype(BF16), m, v
 
 
+def update(sq_ref, *refs):
+    count = 4 * L * 2 * BG * FF + 4 * L * BD * D
+    squares = jnp.sum(jnp.sum(sq_ref[...], axis=0, keepdims=True), axis=1, keepdims=True)
+    factor = jnp.minimum(1.0, 0.5 * lax.rsqrt(squares / count + 1e-30))
+    for n in range(3):
+        w, m, v, g = (refs[4 * n + k] for k in range(4))
+        new = adamw(w[...].astype(F32), m[...], v[...], g[...].astype(F32) * factor[None])
+        for k in range(3):
+            refs[12 + 3 * k + n][...] = new[k]
+
+
+def updated(sq, weights, m, v, gradients):
+    parts = 6
+    tiles = [pl.BlockSpec((1, w.shape[1] // parts, w.shape[2]), lambda i, j: (i, j, 0)) for w in weights]
+    arrays = [a for four in zip(weights, m, v, gradients, strict=True) for a in four]
+    like = lambda dtype: [jax.ShapeDtypeStruct(w.shape, dtype) for w in weights]
+    return pl.pallas_call(
+        update,
+        grid=(L, parts),
+        in_specs=[pl.BlockSpec((8, 128), lambda i, j: (0, 0))] + [t for t in tiles for _ in range(4)],
+        out_specs=tiles * 3,
+        out_shape=like(BF16) + like(F32) + like(F32),
+        compiler_params=pltpu.CompilerParams(vmem_limit_bytes=60 * 2**20),
+        name="adamw",
+    )(sq, *arrays)
+
+
 def solution(mesh):
     def step(x, dy, *arrays):
         weights, m, v = (arrays[i : i + 3] for i in (0, 3, 6))
         *gradients, sq = fused(x[0], dy[0], *weights)
-        squares = jnp.sum(sq)
-        count = lax.psum(1, "dp") * sum(g.size for g in gradients)
-        factor = jnp.minimum(1.0, 0.5 * lax.rsqrt(squares / count + 1e-30))
-        new = [adamw(w.astype(F32), m, v, g.astype(F32) * factor) for w, m, v, g in zip(weights, m, v, gradients, strict=True)]
-        return tuple(one[which] for which in range(3) for one in new)
+        return tuple(updated(sq, weights, m, v, gradients))
 
     states, cut = P(("rep", "dp"), None, None), P(None, "dp", None)
     return jax.shard_map(

time: 644 us -> 626 us (0.972)
  other arithmetic: 63 us -> 0 us
  Pallas kernels: 579 us -> 624 us
    convert_element_type x2 -> x0, other arithmetic: 61.7 us -> none  [adamw(): return ((w - 0.02 * step).astype(BF16), m, v)]
    pallas_call x0 -> x1, Pallas kernels: none -> 56.7 us  [updated(): pl.pallas_call(update, grid=(L, parts), in_specs=[pl.BlockSpec((8, 128),...]
    pallas_call x1, Pallas kernels: 579 us -> 567 us  [fused(): pl.pallas_call(mega, out_shape=outs, in_specs=[ANY] * 5, out_specs=specs,...]
where the time goes in v4:
time: 626 us; the launch traced here: 624 us
  Pallas kernels  624 us (100%)
    pallas_call x1, Pallas kernels, fused(): pl.pallas_call(mega, out_shape=outs, in_specs=[ANY] * 5, out_specs=specs,...  567 us
    pallas_call x1, Pallas kernels, updated(): pl.pallas_call(update, grid=(L, parts), in_specs=[pl.BlockSpec((8, 128),...  56.7 us

profile of v4, /device:TPU:0, one launch (start us, length us, event | category | flops | bytes accessed | tf_op | source)
XLA Modules:
  0.0 624.4 jit_solution(4730236513878581901)
XLA Ops:
  0.6 567.0 %step.1 = (bf16[2,288,4608]{2,1,0:T(8,128)(2,1)}, bf16[2,288,4608]{2,1,0:T(8,128)(2,1)}, bf16[2,1152,1152]{2,1,0:T(8,128)(2,1)}, f32[8,128]{1,0:T(8,128)}, bf16[...) custom-call(bf16[2048,1152]{1,0:T(8,128)(2,1)} %bitcast.2, ...), custom_call_target="tpu_custom_call" | custom-call | tf_op jit(solution)/shard_map/step/pallas_call | solution.py:543
  567.6 56.7 %adamw.1 = (bf16[2,288,4608]{2,1,0:T(8,128)(2,1)}, bf16[2,288,4608]{2,1,0:T(8,128)(2,1)}, bf16[2,1152,1152]{2,1,0:T(8,128)(2,1)}, f32[2,288,4608]{2,1,0:T(8,128)...) custom-call(f32[8,128]{1,0:T(8,128)} %get-tuple-element.13.sq_ref, ...), custom_call_target="tpu_custom_call" | custom-call | tf_op jit(solution)/shard_map/adamw/pallas_call | solution.py:582

commit v5 on v4

--- a/solution.py
+++ b/solution.py
@@ -575,7 +575,7 @@
 
 
 def updated(sq, weights, m, v, gradients):
-    parts = 6
+    parts = 9
     tiles = [pl.BlockSpec((1, w.shape[1] // parts, w.shape[2]), lambda i, j: (i, j, 0)) for w in weights]
     arrays = [a for four in zip(weights, m, v, gradients, strict=True) for a in four]
     like = lambda dtype: [jax.ShapeDtypeStruct(w.shape, dtype) for w in weights]

time: 626 us -> 628 us (level)
  no operation moved by 1% of the time
where the time goes in v5:
time: 628 us; the launch traced here: 626 us
  Pallas kernels  625 us (100%)
    pallas_call x1, Pallas kernels, fused(): pl.pallas_call(mega, out_shape=outs, in_specs=[ANY] * 5, out_specs=specs,...  567 us
    pallas_call x1, Pallas kernels, updated(): pl.pallas_call(update, grid=(L, parts), in_specs=[pl.BlockSpec((8, 128),...  58.5 us

profile of v5, /device:TPU:0, one launch (start us, length us, event | category | flops | bytes accessed | tf_op | source)
XLA Modules:
  0.0 626.3 jit_solution(1731797325609927618)
XLA Ops:
  0.6 567.0 %step.1 = (bf16[2,288,4608]{2,1,0:T(8,128)(2,1)}, bf16[2,288,4608]{2,1,0:T(8,128)(2,1)}, bf16[2,1152,1152]{2,1,0:T(8,128)(2,1)}, f32[8,128]{1,0:T(8,128)}, bf16[...) custom-call(bf16[2048,1152]{1,0:T(8,128)(2,1)} %bitcast.2, ...), custom_call_target="tpu_custom_call" | custom-call | tf_op jit(solution)/shard_map/step/pallas_call | solution.py:543
  567.6 58.5 %adamw.1 = (bf16[2,288,4608]{2,1,0:T(8,128)(2,1)}, bf16[2,288,4608]{2,1,0:T(8,128)(2,1)}, bf16[2,1152,1152]{2,1,0:T(8,128)(2,1)}, f32[2,288,4608]{2,1,0:T(8,128)...) custom-call(f32[8,128]{1,0:T(8,128)} %get-tuple-element.13.sq_ref, ...), custom_call_target="tpu_custom_call" | custom-call | tf_op jit(solution)/shard_map/adamw/pallas_call | solution.py:582
